TPU v7x, 32 devices: a whole 2x2x4 slice. The times are simulated.
32 devices in a mesh: dp: 4 (over z), replica: 2 (over y), fsdp: 4 (over x, core).
Axes of the slice: x: 2, y: 2, z: 4, core: 2. Of those that a mesh axis runs over, the one named last changes fastest.
Arguments:
- x_tokens: bfloat16 [131072, 768], P(('dp', 'replica', 'fsdp'))
- dy_tokens: bfloat16 [131072, 768], P(('dp', 'replica', 'fsdp'))
- w_gate: bfloat16 [2, 768, 3072], P(None, 'fsdp')
- w_up: bfloat16 [2, 768, 3072], P(None, 'fsdp')
- w_down: bfloat16 [2, 3072, 768], P(None, 'fsdp')
- norm_gain: float32 [2, 768], replicated
Outputs:
- output 1: bfloat16 [131072, 768], P(('dp', 'replica', 'fsdp'))
- output 2: float32 [2, 768, 3072], P(None, 'fsdp')
- output 3: float32 [2, 768, 3072], P(None, 'fsdp')
- output 4: float32 [2, 3072, 768], P(None, 'fsdp')
- output 5: float32 [2, 768], replicated
All inputs are finite; a program needn't handle non-finite values.
Results may differ from a plain program's by a relative error of at most 0.0148433.
Values are sent between devices in bfloat16 or wider.
A program may use at most 1 GiB of HBM per device.

v0:
```python
import jax
import jax.numpy as jnp
from jax import lax
from jax.sharding import PartitionSpec as P

NORM_EPS = 1e-6
TOKEN_AXES = ("dp", "replica", "fsdp")
COPY_AXES = ("dp", "replica")
CONTRACT_ROWS = (((0,), (0,)), ((), ()))
CONTRACT_COLS = (((1,), (1,)), ((), ()))


def layer_forward(hidden, w_gate, w_up, w_down, gain_row):
    hidden_f = hidden.astype(jnp.float32)
    inv_rms = lax.rsqrt(jnp.mean(hidden_f * hidden_f, axis=-1, keepdims=True) + NORM_EPS)
    normed = (hidden_f * inv_rms * gain_row).astype(jnp.bfloat16)
    gate_act = jnp.dot(normed, w_gate, preferred_element_type=jnp.float32).astype(jnp.bfloat16)
    up_act = jnp.dot(normed, w_up, preferred_element_type=jnp.float32).astype(jnp.bfloat16)
    prod_act = (jax.nn.silu(gate_act.astype(jnp.float32)) * up_act.astype(jnp.float32)).astype(jnp.bfloat16)
    layer_out = (hidden_f + jnp.dot(prod_act, w_down, preferred_element_type=jnp.float32)).astype(jnp.bfloat16)
    return layer_out, (hidden, inv_rms, normed, gate_act, up_act, prod_act)


def layer_backward(cot_out, saved_vals, w_gate, w_up, w_down, gain_row):
    hidden, inv_rms, normed, gate_act, up_act, prod_act = saved_vals
    dw_down = lax.dot_general(prod_act, cot_out, CONTRACT_ROWS, preferred_element_type=jnp.float32)
    d_prod = lax.dot_general(cot_out, w_down, CONTRACT_COLS, preferred_element_type=jnp.float32).astype(jnp.bfloat16).astype(jnp.float32)
    gate_f = gate_act.astype(jnp.float32)
    sig_gate = jax.nn.sigmoid(gate_f)
    d_gate = (d_prod * up_act.astype(jnp.float32) * sig_gate * (1.0 + gate_f * (1.0 - sig_gate))).astype(jnp.bfloat16)
    d_up = (d_prod * gate_f * sig_gate).astype(jnp.bfloat16)
    dw_gate = lax.dot_general(normed, d_gate, CONTRACT_ROWS, preferred_element_type=jnp.float32)
    dw_up = lax.dot_general(normed, d_up, CONTRACT_ROWS, preferred_element_type=jnp.float32)
    d_normed = (lax.dot_general(d_gate, w_gate, CONTRACT_COLS, preferred_element_type=jnp.float32) + lax.dot_general(d_up, w_up, CONTRACT_COLS, preferred_element_type=jnp.float32)).astype(jnp.bfloat16).astype(jnp.float32)
    hidden_f = hidden.astype(jnp.float32)
    d_gain = jnp.sum(d_normed * hidden_f * inv_rms, axis=0)
    scaled = d_normed * gain_row
    d_hidden = cot_out.astype(jnp.float32) + inv_rms * scaled - hidden_f * (inv_rms * inv_rms * inv_rms) * jnp.mean(scaled * hidden_f, axis=-1, keepdims=True)
    return d_hidden.astype(jnp.bfloat16), dw_gate, dw_up, dw_down, d_gain


def solution(mesh):
    tok_spec = P(TOKEN_AXES, None)
    shard_spec = P(None, "fsdp", None)
    full_spec = P(None, None)

    def gather_layer(w_gate_sh, w_up_sh, w_down_sh, layer_idx):
        gate_full = lax.all_gather(w_gate_sh[layer_idx], "fsdp", axis=0, tiled=True)
        up_full = lax.all_gather(w_up_sh[layer_idx], "fsdp", axis=0, tiled=True)
        down_full = lax.all_gather(w_down_sh[layer_idx], "fsdp", axis=0, tiled=True)
        return gate_full, up_full, down_full

    def reduce_grad(grad_local):
        grad_shard = lax.psum_scatter(grad_local, "fsdp", scatter_dimension=0, tiled=True)
        return lax.psum(grad_shard, COPY_AXES)

    def device_step(x_local, dy_local, w_gate_sh, w_up_sh, w_down_sh, norm_gain):
        num_layers = w_gate_sh.shape[0]
        hidden = x_local
        saved_list = []
        for layer_idx in range(num_layers):
            gate_full, up_full, down_full = gather_layer(w_gate_sh, w_up_sh, w_down_sh, layer_idx)
            hidden, saved_vals = layer_forward(hidden, gate_full, up_full, down_full, norm_gain[layer_idx])
            saved_list.append(saved_vals)
        cot_out = dy_local
        grad_map = {}
        for layer_idx in reversed(range(num_layers)):
            gate_full, up_full, down_full = gather_layer(w_gate_sh, w_up_sh, w_down_sh, layer_idx)
            cot_out, dw_gate, dw_up, dw_down, d_gain = layer_backward(cot_out, saved_list[layer_idx], gate_full, up_full, down_full, norm_gain[layer_idx])
            grad_map[layer_idx] = (reduce_grad(dw_gate), reduce_grad(dw_up), reduce_grad(dw_down), d_gain)
        stacked = [jnp.stack([grad_map[layer_idx][part_idx] for layer_idx in range(num_layers)]) for part_idx in range(4)]
        gain_sum = lax.psum(stacked[3], TOKEN_AXES)
        return (hidden, stacked[0], stacked[1], stacked[2], gain_sum)

    return jax.shard_map(device_step, mesh=mesh, in_specs=(tok_spec, tok_spec, shard_spec, shard_spec, shard_spec, full_spec), out_specs=(tok_spec, shard_spec, shard_spec, shard_spec, full_spec), check_vma=False)
```

profile of v0, /device:TPU:0, one launch (start us, length us, event | category | flops | bytes accessed | tf_op | source)
XLA Modules:
  0.0 1326.2 jit_solution(422941027364089286)
XLA Ops:
  7.2 0.0 all-gather.13.cloned.1.call-start
  7.2 3.3 fusion.65
  10.6 0.0 all-gather.13.cloned.1.call-update
  10.6 0.0 all-gather.15.cloned.1.call-start
  10.6 3.2 fusion.66
  13.8 0.0 all-gather.15.cloned.1.call-update
  13.8 0.0 all-gather.17.cloned.1.call-start
  13.9 1.6 fusion.64
  15.5 0.0 all-gather.17.cloned.1.call-update
  15.5 0.0 all-gather.23.cloned.1.call-start
  15.5 0.5 all-gather.23.cloned.1.call-update
  16.1 0.0 all-gather.21.cloned.1.call-start
  16.1 0.5 all-gather.21.cloned.1.call-update
  16.7 0.0 all-gather.19.cloned.1.call-start
  16.7 0.5 all-gather.19.cloned.1.call-update
  17.2 0.0 reduce-scatter.9.cloned.1.call-start
  17.3 8.6 copy.11
  25.8 0.6 slice_reduce_fusion
  26.5 4.1 fusion.24
  30.6 8.7 copy.13
  39.3 11.5 all-gather.13.cloned.1.call-done
  50.8 27.9 %convolution_convert_fusion.5 = bf16[4096,3072]{1,0:T(8,128)(2,1)} fusion(bf16[1,768,3072]{2,1,0:T(8,128)(2,1)} %all-gather.13.cloned.1.call-done, bf16[4096,768]{0,1:T(8,128)(2,1)} %copy.11, f32[768]{0:T(1024)S(1)} %get-tuple-element.13, f32[4096]{0:T(1024)S(1)} %add_rsqrt_fusion.1), kind=kOutput, calls=%fused_computation.43 | convolution fusion | flops 19352518656 | bytes 36195328 | tf_op jit(solution)/shard_map/dot_general | solution.py:17
  78.7 11.6 all-gather.15.cloned.1.call-done
  90.3 40.3 %fusion = (bf16[4096,3072]{1,0:T(8,128)(2,1)}, bf16[4096,3072]{1,0:T(8,128)(2,1)}) fusion(bf16[4096,3072]{1,0:T(8,128)(2,1)} %convolution_convert_fusion.5, bf16[1,768,3072]{2,1,0:T(8,128)(2,1)} %all-gather.15.cloned.1.call-done, bf16[4096,768]{0,1:T(8,128)(2,1)} %copy.11, f32[768]{0:T(1024)S(1)} %get-tuple-element.13, f32[4096]{0:T(1024)S(1)} %add_rsqrt_fusion.1), kind=kOutput, calls=%fused_computation.12 | convolution fusion | flops 19453181952 | bytes 86526976 | tf_op jit(solution)/shard_map/dot_general | solution.py:18
  130.6 27.4 %fusion.30 = (f32[4096]{0:T(1024)S(1)}, bf16[4096,768]{0,1:T(8,128)(2,1)}) fusion(bf16[4096,3072]{1,0:T(8,128)(2,1)} %get-tuple-element.33, bf16[1,3072,768]{2,1,0:T(8,128)(2,1)} %all-gather.17.cloned.1.call-done, bf16[4096,768]{0,1:T(8,128)(2,1)} %copy.11), kind=kOutput, calls=%fused_computation.59 | convolution fusion | flops 19346223104 | bytes 42483712 | tf_op jit(solution)/shard_map/dot_general | solution.py:20
  158.1 0.6 multiply_multiply_fusion
  158.7 9.3 all-gather.23.cloned.1.call-done
  167.9 26.9 %convolution_convert_fusion.1 = bf16[4096,3072]{1,0:T(8,128)(2,1)} fusion(bf16[4096,768]{1,0:T(8,128)(2,1)} %param.7, bf16[1,3072,768]{2,1,0:T(8,128)(2,1)} %all-gather.23.cloned.1.call-done), kind=kOutput, calls=%fused_computation.39 | convolution fusion | flops 19339935744 | bytes 36175872 | tf_op jit(solution)/shard_map/dot_general | solution.py:27
  194.8 12.4 all-gather.21.cloned.1.call-done
  207.3 28.4 %convolution_convert_fusion.2 = bf16[4096,3072]{1,0:T(8,128)(2,1)} fusion(bf16[1,768,3072]{2,1,0:T(8,128)(2,1)} %all-gather.21.cloned.1.call-done, bf16[4096,768]{0,1:T(8,128)(2,1)} %get-tuple-element.36, f32[768]{0:T(1024)S(1)} %copy-done.5, f32[4096]{0:T(1024)S(1)} %get-tuple-element.32), kind=kOutput, calls=%fused_computation.40 | convolution fusion | flops 19352518656 | bytes 36195328 | tf_op jit(solution)/shard_map/dot_general | solution.py:18
  235.7 11.0 all-gather.19.cloned.1.call-done
  246.6 58.6 %fusion.19 = (bf16[4096,3072]{1,0:T(8,128)(2,1)}, bf16[4096,3072]{1,0:T(8,128)(2,1)}, bf16[4096,3072]{1,0:T(8,128)(2,1)}) fusion(bf16[4096,3072]{1,0:T(8,128)(2,1)} %convolution_convert_fusion.1, bf16[4096,3072]{1,0:T(8,128)(2,1)} %convolution_convert_fusion.2, bf16[1,768,3072]{2,1,0:T(8,128)(2,1)} %all-gather.19.cloned.1.call-done, ...), kind=kOutput, calls=%fused_computation.31 | convolution fusion | flops 19591593984 | bytes 136858624 | tf_op jit(solution)/shard_map/dot_general | solution.py:17
  305.3 24.9 %fusion.54 = f32[768,3072]{1,0:T(8,128)} fusion(bf16[4096,3072]{1,0:T(8,128)(2,1)} %get-tuple-element.23, bf16[4096,768]{0,1:T(8,128)(2,1)S(1)} %copy-done, f32[768]{0:T(1024)S(1)} %copy-done.5, f32[4096]{0:T(1024)S(1)} %get-tuple-element.32), kind=kOutput, calls=%fused_computation.94 | convolution fusion | flops 19339935744 | bytes 40913920 | tf_op jit(solution)/shard_map/dot_general | solution.py:32
  330.1 0.0 reduce-scatter.9.cloned.1.call-update
  330.1 0.0 reduce-scatter.7.cloned.1.call-start
  330.2 26.5 %fusion.42 = f32[4096,768]{0,1:T(8,128)} fusion(bf16[4096,3072]{1,0:T(8,128)(2,1)} %get-tuple-element.23, bf16[1,768,3072]{2,1,0:T(8,128)(2,1)} %all-gather.19.cloned.1.call-done), kind=kOutput, calls=%fused_computation.76 | convolution fusion | flops 19327352832 | bytes 42467328 | tf_op jit(solution)/shard_map/dot_general | solution.py:34
  356.7 28.9 %fusion.37 = (f32[768]{0:T(1024)}, f32[4096]{0:T(1024)S(1)}, bf16[4096,768]{0,1:T(8,128)(2,1)S(1)}) fusion(bf16[4096,768]{0,1:T(8,128)(2,1)} %get-tuple-element.36, f32[4096]{0:T(1024)S(1)} %get-tuple-element.32, f32[768]{0:T(1024)S(1)} %copy-done.5, f32[4096,768]{0,1:T(8,128)} %fusion.42, bf16[4096,3072]{1,0:T(8,128)(2,1)} %get-tuple-element.22, ...), kind=kOutput, calls=%fused_computation.66 | convolution fusion | flops 19358806016 | bytes 55089152 | tf_op jit(solution)/shard_map/dot_general | solution.py:34
  385.7 6.5 fusion.23
  392.2 52.0 %fusion.13 = (bf16[4096,3072]{1,0:T(8,128)(2,1)}, bf16[4096,3072]{1,0:T(8,128)(2,1)}) fusion(bf16[4096,3072]{1,0:T(8,128)(2,1)} %convolution_convert_fusion.5, bf16[4096,3072]{1,0:T(8,128)(2,1)} %get-tuple-element.34, bf16[4096,768]{0,1:T(8,128)(2,1)} %fusion.23, bf16[1,3072,768]{2,1,0:T(8,128)(2,1)} %all-gather.17.cloned.1.call-done), kind=kOutput, calls=%fused_computation.25 | convolution fusion | flops 19541262336 | bytes 111673344 | tf_op jit(solution)/shard_map/dot_general | solution.py:27
  444.2 26.6 %fusion.60 = f32[768,3072]{1,0:T(8,128)} fusion(bf16[4096,3072]{1,0:T(8,128)(2,1)} %get-tuple-element.21, bf16[4096,768]{0,1:T(8,128)(2,1)} %copy.11, f32[768]{0:T(1024)S(1)} %copy-done.12, f32[4096]{0:T(1024)S(1)} %copy-done.8), kind=kOutput, calls=%fused_computation.96 | convolution fusion | flops 19339935744 | bytes 40913920 | tf_op jit(solution)/shard_map/dot_general | solution.py:32
  470.8 0.0 reduce-scatter.7.cloned.1.call-update
  470.8 0.0 reduce-scatter.13.cloned.1.call-start
  470.9 26.6 %fusion.52 = f32[768,3072]{1,0:T(8,128)} fusion(bf16[4096,3072]{1,0:T(8,128)(2,1)} %get-tuple-element.22, bf16[4096,768]{0,1:T(8,128)(2,1)} %get-tuple-element.36, f32[768]{0:T(1024)S(1)} %copy-done.6, f32[4096]{0:T(1024)S(1)} %copy-done.3), kind=kOutput, calls=%fused_computation.93 | convolution fusion | flops 19339935744 | bytes 40913920 | tf_op jit(solution)/shard_map/dot_general | solution.py:33
  497.6 0.0 reduce-scatter.11.cloned.1.call-start
  497.6 26.5 %fusion.58 = f32[768,3072]{1,0:T(8,128)} fusion(bf16[4096,3072]{1,0:T(8,128)(2,1)} %get-tuple-element.20, bf16[4096,768]{0,1:T(8,128)(2,1)} %copy.11, f32[768]{0:T(1024)S(1)} %copy-done.12, f32[4096]{0:T(1024)S(1)} %copy-done.8), kind=kOutput, calls=%fused_computation.95 | convolution fusion | flops 19339935744 | bytes 40913920 | tf_op jit(solution)/shard_map/dot_general | solution.py:33
  524.2 0.0 reduce-scatter.17.cloned.1.call-start
  524.2 26.7 %fusion.68 = f32[3072,768]{1,0:T(8,128)} fusion(bf16[4096,3072]{1,0:T(8,128)(2,1)} %get-tuple-element.24, bf16[4096,768]{1,0:T(8,128)(2,1)} %param.7), kind=kOutput, calls=%fused_computation.101 | convolution fusion | flops 19327352832 | bytes 40894464 | tf_op jit(solution)/shard_map/dot_general | solution.py:26
  550.9 0.0 reduce-scatter.15.cloned.1.call-start
  551.0 26.8 %fusion.67 = f32[3072,768]{1,0:T(8,128)} fusion(bf16[4096,3072]{1,0:T(8,128)(2,1)} %get-tuple-element.33, bf16[4096,768]{0,1:T(8,128)(2,1)} %fusion.23), kind=kOutput, calls=%fused_computation.100 | convolution fusion | flops 19327352832 | bytes 40894464 | tf_op jit(solution)/shard_map/dot_general | solution.py:26
  577.8 0.0 all-reduce.3.cloned.1.call-start
  577.8 0.0 reduce-scatter.9.cloned.1.call-done
  577.9 0.0 reduce-scatter.7.cloned.1.call-done
  577.9 49.9 %reduce-scatter.13.cloned.1.call-done = f32[192,3072]{1,0:T(8,128)} async-done(((f32[768,3072]{1,0:T(8,128)}), f32[192,3072]{1,0:T(8,128)}) %reduce-scatter.13.cloned.1.call-update) | async-done | bytes 2359312 | tf_op jit(solution)/shard_map/reduce_scatter | solution.py:54
  627.8 79.5 %reduce-scatter.11.cloned.1.call-done = f32[192,3072]{1,0:T(8,128)} async-done(((f32[768,3072]{1,0:T(8,128)}), f32[192,3072]{1,0:T(8,128)}) %reduce-scatter.11.cloned.1.call-update) | async-done | bytes 2359312 | tf_op jit(solution)/shard_map/reduce_scatter | solution.py:54
  707.3 79.7 %reduce-scatter.17.cloned.1.call-done = f32[768,768]{1,0:T(8,128)} async-done(((f32[3072,768]{1,0:T(8,128)}), f32[768,768]{1,0:T(8,128)}) %reduce-scatter.17.cloned.1.call-update) | async-done | bytes 2359312 | tf_op jit(solution)/shard_map/reduce_scatter | solution.py:54
  787.0 79.6 %reduce-scatter.15.cloned.1.call-done = f32[768,768]{1,0:T(8,128)} async-done(((f32[3072,768]{1,0:T(8,128)}), f32[768,768]{1,0:T(8,128)}) %reduce-scatter.15.cloned.1.call-update) | async-done | bytes 2359312 | tf_op jit(solution)/shard_map/reduce_scatter | solution.py:54
  866.6 26.4 %fusion.33 = bf16[4096,768]{0,1:T(8,128)(2,1)} fusion(bf16[4096,768]{0,1:T(8,128)(2,1)} %get-tuple-element.36, bf16[4096,3072]{1,0:T(8,128)(2,1)} %get-tuple-element.24, bf16[1,3072,768]{2,1,0:T(8,128)(2,1)} %all-gather.23.cloned.1.call-done), kind=kOutput, calls=%fused_computation.62 | convolution fusion | flops 19336790016 | bytes 42467328 | tf_op jit(solution)/shard_map/dot_general | solution.py:20
  893.0 8.8 copy.18
  901.8 24.6 %fusion.49 = f32[4096,768]{0,1:T(8,128)S(1)} fusion(bf16[4096,3072]{1,0:T(8,128)(2,1)} %get-tuple-element.21, bf16[1,768,3072]{2,1,0:T(8,128)(2,1)} %all-gather.13.cloned.1.call-done), kind=kOutput, calls=%fused_computation.83 | convolution fusion | flops 19327352832 | bytes 42467328 | tf_op jit(solution)/shard_map/dot_general | solution.py:34
  926.4 25.8 %fusion.29 = f32[768]{0:T(1024)S(1)} fusion(bf16[4096,768]{0,1:T(8,128)(2,1)S(1)} %bitcast.65, f32[4096]{0:T(1024)S(1)} %copy-done.9, f32[4096,768]{0,1:T(8,128)S(1)} %fusion.49, bf16[4096,3072]{1,0:T(8,128)(2,1)} %get-tuple-element.20, bf16[1,768,3072]{2,1,0:T(8,128)(2,1)} %all-gather.15.cloned.1.call-done), kind=kOutput, calls=%fused_computation.58 | convolution fusion | flops 19349372928 | bytes 48778240 | tf_op jit(solution)/shard_map/dot_general | solution.py:34
  952.3 41.1 %psum.55 = f32[2,768]{1,0:T(2,128)} all-reduce(f32[2,768]{1,0:T(2,128)S(1)} %pad_maximum_fusion.3), channel_id=1, replica_groups=mesh['dp'=4,'replica'=2,'fsdp'=4] {'dp','replica','fsdp'}, use_global_device_ids=true, to_apply=%region_17.18 | all-reduce | flops 1536 | bytes 12288 | tf_op jit(solution)/shard_map/psum | solution.py:72
  993.4 312.3 %all-reduce.3.cloned.1.call-done = (f32[1,192,3072]{2,1,0:T(8,128)}, f32[1,192,3072]{2,1,0:T(8,128)}, f32[1,192,3072]{2,1,0:T(8,128)}, f32[1,192,3072]{2,1,0:T(8...) async-done(((f32[1,192,3072]{2,1,0:T(8,128)}, f32[1,192,3072]{2,1,0:T(8,128)}, f32[1,192,3072]{2,1,0:T(8,128)}, f32[1,192,3072]{2,1,0:T(8,128)}, ...) | async-done | bytes 14155792 | tf_op jit(solution)/shard_map/psum | solution.py:55
  1305.7 4.9 pad_maximum_fusion.2
  1310.6 8.7 pad_maximum_fusion
  (54 shorter events, 0.2 us)
Async XLA Ops:
  7.2 6.7 copy-start.1
  7.2 43.6 %all-gather.13.cloned.1.call-start = ((), (), s32[]{:S(2)}) async-start(), calls=%async_computation.12 | async-start | bytes 5898240 | tf_op jit(solution)/shard_map/all_gather | solution.py:48
  10.6 79.7 %all-gather.15.cloned.1.call-start = ((), (), s32[]{:S(2)}) async-start(), calls=%async_computation.13 | async-start | bytes 5898240 | tf_op jit(solution)/shard_map/all_gather | solution.py:49
  13.8 12.0 copy-start.10
  13.8 116.8 %all-gather.17.cloned.1.call-start = ((), (), s32[]{:S(2)}) async-start(), calls=%async_computation.14 | async-start | bytes 5898240 | tf_op jit(solution)/shard_map/all_gather | solution.py:50
  15.5 152.5 %all-gather.23.cloned.1.call-start = ((), (), s32[]{:S(2)}) async-start(), calls=%async_computation.17 | async-start | bytes 5898240 | tf_op jit(solution)/shard_map/all_gather | solution.py:50
  16.1 191.2 %all-gather.21.cloned.1.call-start = ((), (), s32[]{:S(2)}) async-start(), calls=%async_computation.16 | async-start | bytes 5898240 | tf_op jit(solution)/shard_map/all_gather | solution.py:49
  16.7 230.0 %all-gather.19.cloned.1.call-start = ((), (), s32[]{:S(2)}) async-start(), calls=%async_computation.15 | async-start | bytes 5898240 | tf_op jit(solution)/shard_map/all_gather | solution.py:48
  17.2 560.6 %reduce-scatter.9.cloned.1.call-start = ((), (), s32[]{:S(2)}) async-start(), calls=%async_computation.7 | async-start | bytes 11796480 | tf_op jit(solution)/shard_map/reduce_scatter | solution.py:54
  26.4 63.8 %copy-start.11 = (f32[768]{0:T(1024)}, f32[768]{0:T(1024)S(1)}, u32[]{:S(2)}) copy-start(f32[768]{0:T(1024)S(1)} %get-tuple-element.13) | copy-start | bytes 9220
  30.5 59.7 %copy-start.7 = (f32[4096]{0:T(1024)}, f32[4096]{0:T(1024)S(1)}, u32[]{:S(2)}) copy-start(f32[4096]{0:T(1024)S(1)} %add_rsqrt_fusion.1) | copy-start | bytes 49156
  158.7 227.0 %copy-start.2 = (f32[4096]{0:T(1024)}, f32[4096]{0:T(1024)S(1)}, u32[]{:S(2)}) copy-start(f32[4096]{0:T(1024)S(1)} %get-tuple-element.32) | copy-start | bytes 49156
  158.7 48.6 %copy-start.5 = (f32[768]{0:T(1024)S(1)}, f32[768]{0:T(1024)}, u32[]{:S(2)}) copy-start(f32[768]{0:T(1024)} %get-tuple-element.12) | copy-start | bytes 9220
  246.6 58.6 %copy-start = (bf16[4096,768]{0,1:T(8,128)(2,1)S(1)}, bf16[4096,768]{0,1:T(8,128)(2,1)}, u32[]{:S(2)}) copy-start(bf16[4096,768]{0,1:T(8,128)(2,1)} %get-tuple-element.36) | copy-start | bytes 18874372
  330.1 247.7 %reduce-scatter.7.cloned.1.call-start = ((), (), s32[]{:S(2)}) async-start(), calls=%async_computation.6 | async-start | bytes 11796480 | tf_op jit(solution)/shard_map/reduce_scatter | solution.py:54
  330.2 55.5 %slice-start.2 = ((s8[6291456]{0:T(1024)(128)(4,1)}), s8[4194304]{0:T(1024)(128)(4,1)S(1)}, s32[]{:S(2)}) async-start(s8[6291456]{0:T(1024)(128)(4,1)} %bitcast.66), calls=%async_computation.21 | async-start | bytes 8388608
  330.2 55.5 %slice-start.4 = ((s8[6291456]{0:T(1024)(128)(4,1)}), s8[4194304]{0:T(1024)(128)(4,1)S(1)}, s32[]{:S(2)}) async-start(s8[6291456]{0:T(1024)(128)(4,1)} %bitcast.68), calls=%async_computation.23 | async-start | bytes 8388608
  356.7 28.9 %slice-start.3 = ((s8[6291456]{0:T(1024)(128)(4,1)}), s8[2097152]{0:T(1024)(128)(4,1)S(1)}, s32[]{:S(2)}) async-start(s8[6291456]{0:T(1024)(128)(4,1)} %bitcast.66), calls=%async_computation.22 | async-start | bytes 4194304
  356.7 29.0 %slice-start.5 = ((s8[6291456]{0:T(1024)(128)(4,1)}), s8[2097152]{0:T(1024)(128)(4,1)S(1)}, s32[]{:S(2)}) async-start(s8[6291456]{0:T(1024)(128)(4,1)} %bitcast.68), calls=%async_computation.24 | async-start | bytes 4194304
  356.7 29.0 %copy-start.4 = (f32[4096]{0:T(1024)S(1)}, f32[4096]{0:T(1024)}, u32[]{:S(2)}) copy-start(f32[4096]{0:T(1024)} %get-tuple-element.31) | copy-start | bytes 49156
  392.2 52.0 %copy-start.8 = (f32[4096]{0:T(1024)S(1)}, f32[4096]{0:T(1024)}, u32[]{:S(2)}) copy-start(f32[4096]{0:T(1024)} %copy-done.7) | copy-start | bytes 49156
  392.2 52.0 %copy-start.12 = (f32[768]{0:T(1024)S(1)}, f32[768]{0:T(1024)}, u32[]{:S(2)}) copy-start(f32[768]{0:T(1024)} %copy-done.11) | copy-start | bytes 9220
  444.2 26.7 %copy-start.3 = (f32[4096]{0:T(1024)S(1)}, f32[4096]{0:T(1024)}, u32[]{:S(2)}) copy-start(f32[4096]{0:T(1024)} %copy-done.2) | copy-start | bytes 49156
  444.2 26.7 %copy-start.6 = (f32[768]{0:T(1024)S(1)}, f32[768]{0:T(1024)}, u32[]{:S(2)}) copy-start(f32[768]{0:T(1024)} %get-tuple-element.12) | copy-start | bytes 9220
  470.8 156.9 %reduce-scatter.13.cloned.1.call-start = ((), (), s32[]{:S(2)}) async-start(), calls=%async_computation.9 | async-start | bytes 11796480 | tf_op jit(solution)/shard_map/reduce_scatter | solution.py:54
  497.6 209.8 %reduce-scatter.11.cloned.1.call-start = ((), (), s32[]{:S(2)}) async-start(), calls=%async_computation.8 | async-start | bytes 11796480 | tf_op jit(solution)/shard_map/reduce_scatter | solution.py:54
  524.2 262.9 %reduce-scatter.17.cloned.1.call-start = ((), (), s32[]{:S(2)}) async-start(), calls=%async_computation.11 | async-start | bytes 11796480 | tf_op jit(solution)/shard_map/reduce_scatter | solution.py:54
  550.9 315.7 %reduce-scatter.15.cloned.1.call-start = ((), (), s32[]{:S(2)}) async-start(), calls=%async_computation.10 | async-start | bytes 11796480 | tf_op jit(solution)/shard_map/reduce_scatter | solution.py:54
  577.8 727.9 %all-reduce.3.cloned.1.call-start = ((), (), s32[]{:S(2)}) async-start(), calls=%async_computation.18 | async-start | bytes 28311552 | tf_op jit(solution)/shard_map/psum | solution.py:55
  893.0 8.8 copy-start.13
  893.0 33.4 %slice-start = ((s8[6291456]{0:T(1024)(128)(4,1)}), s8[2097152]{0:T(1024)(128)(4,1)S(1)}, s32[]{:S(2)}) async-start(s8[6291456]{0:T(1024)(128)(4,1)} %bitcast.64), calls=%async_computation.19 | async-start | bytes 4194304
  901.8 24.6 %slice-start.1 = ((s8[6291456]{0:T(1024)(128)(4,1)}), s8[4194304]{0:T(1024)(128)(4,1)S(1)}, s32[]{:S(2)}) async-start(s8[6291456]{0:T(1024)(128)(4,1)} %bitcast.64), calls=%async_computation.20 | async-start | bytes 8388608
  901.8 24.6 %copy-start.9 = (f32[4096]{0:T(1024)S(1)}, f32[4096]{0:T(1024)}, u32[]{:S(2)}) copy-start(f32[4096]{0:T(1024)} %copy-done.7) | copy-start | bytes 49156
Sparse Core Ops, SparseCore 0:
  10.7 40.0 all-gather.12
  52.9 37.3 all-gather.14
  91.8 37.2 all-gather.16
  130.6 37.2 all-gather.22
  169.9 37.3 all-gather.20
  209.3 37.2 all-gather.18
  330.3 77.0 reduce-scatter.8
  471.0 77.0 reduce-scatter.6
  550.7 77.0 reduce-scatter.12
  630.2 77.0 reduce-scatter.10
  709.9 77.0 reduce-scatter.16
  789.5 77.0 reduce-scatter.14
  871.9 433.7 all-reduce.2
where the time goes:
time: 1330 us
  waiting for transfers between devices  659 us (50%)
  matrix products  552 us (42%)
  blocking collectives  41.1 us (3%)
  local copies, waits for them, and re-layouts  34.8 us (3%)
  other arithmetic  24.8 us (2%)
  between operations  14.6 us (1%)
    psum x1, waiting for transfers between devices, reduce_grad(): return lax.psum(grad_shard, COPY_AXES)  312 us
    reduce_scatter x6, waiting for transfers between devices, reduce_grad(): lax.psum_scatter(grad_local, 'fsdp', scatter_dimension=0, tiled=True)  289 us
    dot_general x2, matrix products, layer_forward(): jnp.dot(normed, w_gate, preferred_element_type=jnp.float32)  86.6 us
    dot_general x2, matrix products, layer_backward(): lax.dot_general(cot_out, w_down, CONTRACT_COLS, preferred_element_type=jn...  78.9 us
    dot_general x2, matrix products, layer_forward(): jnp.dot(normed, w_up, preferred_element_type=jnp.float32)  68.7 us
    dot_general x2, matrix products, layer_backward(): lax.dot_general(d_up, w_up, CONTRACT_COLS, preferred_element_type=jnp.flo...  54.7 us
    dot_general x2, matrix products, layer_forward(): jnp.dot(prod_act, w_down, preferred_element_type=jnp.float32)  53.8 us
    dot_general x2, matrix products, layer_backward(): lax.dot_general(prod_act, cot_out, CONTRACT_ROWS, preferred_element_type=...  53.5 us
  transfers between devices with their start and end apart: 13, of which 10 were waited for; matrix products, arithmetic and copies ran while one was open for 39% of the time, Pallas kernels for 0%

commit v1 on v0

v1 whole, which is shorter than its diff:
```python
import jax
import jax.numpy as jnp
from jax import lax
from jax.experimental import pallas as pl
from jax.experimental.pallas import tpu as pltpu
from jax.sharding import PartitionSpec as P

NORM_EPS = 1e-6
TOKEN_AXES = ("dp", "replica", "fsdp")
MESH_ID = pl.DeviceIdType.MESH
BF16 = jnp.bfloat16
F32 = jnp.float32

TOK = 4096
D = 768
FF = 3072
LAYERS = 2
TM = 512
NT = TOK // TM
FT = 512
NF = FF // FT
GR = D // 4
UNITS = LAYERS * NF
TILES = LAYERS * NF
JOBS = 3 * TILES
BLK = (384, 256)
VMEM_MAX = 67043328
O1, O2, O3, O4, O5, O6, O7 = 1, 3, 4, 5, 6, 7, 8
TICKS = JOBS + O7
MAIN = LAYERS * NF * NT
DRAIN = TICKS - 3 * (TILES - 1)


def dot_nn(a, b):
    return lax.dot_general(a, b, (((1,), (0,)), ((), ())), preferred_element_type=F32)


def dot_nt(a, b):
    return lax.dot_general(a, b, (((1,), (1,)), ((), ())), preferred_element_type=F32)


def dot_tn(a, b):
    return lax.dot_general(a, b, (((0,), (0,)), ((), ())), preferred_element_type=F32)


def sigmoid(v):
    return 0.5 * jnp.tanh(0.5 * v) + 0.5


def inv_rms_of(h):
    return lax.rsqrt(jnp.mean(h * h, axis=-1, keepdims=True) + NORM_EPS)


def rows_of(start, size, unit):
    return pl.ds(pl.multiple_of(start, unit), size)


def place():
    shard = lax.axis_index("fsdp")
    return shard, shard // 2, shard % 2, lax.axis_index("replica"), lax.axis_index("dp")


def entry_barrier(partners):
    barrier = pltpu.get_barrier_semaphore()
    for partner in partners:
        pl.semaphore_signal(barrier, inc=1, device_id=partner, device_id_type=MESH_ID)
    pl.semaphore_wait(barrier, len(partners))


def gather_kernel(x_blk, gain_blk, wg_sh, wu_sh, wd_sh, gu_out, h1_out, wgu_hbm, wd_hbm,
                  n_all, acc, wgu, wd, load_sem, send_sem, recv_sem, out_sem):
    step = pl.program_id(0)
    tile = step // NT
    tok = step % NT
    shard, xx, cc, yy, zz = place()
    core_dev = {"fsdp": 2 * xx + (1 - cc)}
    x_dev = {"fsdp": 2 * (1 - xx) + cc}
    y_dev = {"replica": 1 - yy}
    core_sh = 2 * xx + (1 - cc)
    x_sh = 2 * (1 - xx) + cc
    far_sh = 2 * (1 - xx) + (1 - cc)

    def part(unit, owner, half):
        if half is None:
            return wgu.at[unit, rows_of(owner * GR, GR, GR), :], wd.at[unit, rows_of(owner * 128, 128, 128), :]
        return (wgu.at[unit, rows_of(owner * GR + half * 96, 96, 96), :],
                wd.at[unit, rows_of(owner * 128 + half * 64, 64, 64), :])

    def message(unit, kind, owner, half, dev):
        return [pltpu.make_async_remote_copy(src_ref=ref, dst_ref=ref, send_sem=send_sem.at[unit, kind, i],
                                             recv_sem=recv_sem.at[unit, kind, i], device_id=dev,
                                             device_id_type=MESH_ID)
                for i, ref in enumerate(part(unit, owner, half))]

    def send(unit, kind, owner, half, dev):
        for copy in message(unit, kind, owner, half, dev):
            copy.start()

    def arrived(unit, kind, owner, half, dev):
        for copy in message(unit, kind, owner, half, dev):
            copy.wait_recv()

    def load(unit):
        layer = unit // NF
        col = (unit % NF) * 128
        for group in range(4):
            cols = rows_of(group * D + col, 128, 128)
            pltpu.make_async_copy(wg_sh.at[layer, :, cols],
                                  wgu.at[unit, rows_of(shard * GR, GR, GR), pl.ds(group * 128, 128)],
                                  load_sem.at[unit, 0]).start()
            pltpu.make_async_copy(wu_sh.at[layer, :, cols],
                                  wgu.at[unit, rows_of(shard * GR, GR, GR), pl.ds(FT + group * 128, 128)],
                                  load_sem.at[unit, 0]).start()
        pltpu.make_async_copy(wd_sh.at[layer, rows_of(col, 128, 128), :],
                              wd.at[unit, rows_of(shard * 128, 128, 128), :], load_sem.at[unit, 1]).start()

    def send_own(unit):
        own = part(unit, shard, None)
        for i in range(2):
            pltpu.make_async_copy(own[i], own[i], load_sem.at[unit, i]).wait()
        send(unit, 1, shard, yy, x_dev)
        send(unit, 0, shard, None, core_dev)

    def forward_x(unit):
        arrived(unit, 1, x_sh, yy, x_dev)
        send(unit, 2, x_sh, yy, y_dev)
        send(unit, 3, x_sh, yy, core_dev)

    def forward_y(unit):
        arrived(unit, 2, x_sh, 1 - yy, y_dev)
        send(unit, 4, x_sh, 1 - yy, core_dev)

    def outs(unit):
        return (pltpu.make_async_copy(wgu.at[unit], wgu_hbm.at[unit], out_sem.at[unit, 0]),
                pltpu.make_async_copy(wd.at[unit], wd_hbm.at[unit], out_sem.at[unit, 1]))

    def complete(unit):
        arrived(unit, 0, core_sh, None, core_dev)
        arrived(unit, 3, far_sh, yy, core_dev)
        arrived(unit, 4, far_sh, 1 - yy, core_dev)
        for copy in outs(unit):
            copy.start()

    @pl.when(step == 0)
    def _():
        @pl.loop(0, UNITS)
        def _(unit):
            load(unit)

        entry_barrier((core_dev, x_dev, y_dev))

        @pl.loop(0, 4)
        def _(unit):
            send_own(unit)

        forward_x(0)
        forward_y(0)

    @pl.when(jnp.logical_and(step % 4 == 1, step // 4 + 1 < UNITS))
    def _():
        unit = step // 4 + 1

        @pl.when(unit + 3 < UNITS)
        def _():
            send_own(unit + 3)

        forward_x(unit)

    @pl.when(jnp.logical_and(step % 4 == 0, step >= 4))
    def _():
        forward_y(step // 4)

    @pl.when(tok == 0)
    def _():
        complete(tile)

    @pl.when(jnp.logical_and(step % 4 == 3, step // 4 >= NF))
    def _():
        complete(step // 4)

    rows = rows_of(tok * TM, TM, TM)

    @pl.when(tile == 0)
    def _():
        h = x_blk[...].astype(F32)
        n_all[rows, :] = (h * inv_rms_of(h) * gain_blk[0:1, :]).astype(BF16)

    gu = dot_nn(n_all[rows, :], wgu[tile]).astype(BF16)
    gu_out[0] = gu
    gate = gu[:, :FT].astype(F32)
    prod = (gate * sigmoid(gate) * gu[:, FT:].astype(F32)).astype(BF16)
    acc[rows, :] = jnp.where(tile == 0, 0.0, acc[rows, :]) + dot_nn(prod, wd[tile])

    @pl.when(tile == NF - 1)
    def _():
        h1_out[...] = (x_blk[...].astype(F32) + acc[rows, :]).astype(BF16)

    @pl.when(step == NF * NT - 1)
    def _():
        @pl.loop(0, UNITS)
        def _(unit):
            for kind, owner, half, dev in ((0, shard, None, core_dev), (1, shard, yy, x_dev), (2, x_sh, yy, y_dev),
                                           (3, x_sh, yy, core_dev), (4, x_sh, 1 - yy, core_dev)):
                for copy in message(unit, kind, owner, half, dev):
                    copy.wait_send()
            for copy in outs(unit):
                copy.wait()


def forward_gather(x, gain, wg_sh, wu_sh, wd_sh):
    any_spec = pl.BlockSpec(memory_space=pl.ANY)

    def x_index(s):
        return (jnp.where(jnp.logical_or(s // NT == 0, s // NT == NF - 1), s % NT, NT - 1), 0)

    return pl.pallas_call(
        gather_kernel,
        grid=(NF * NT,),
        in_specs=[pl.BlockSpec((TM, D), x_index), pl.BlockSpec((LAYERS, D), lambda s: (0, 0)),
                  any_spec, any_spec, any_spec],
        out_specs=[pl.BlockSpec((1, TM, 2 * FT), lambda s: (s // NT, s % NT, 0)),
                   pl.BlockSpec((TM, D), lambda s: (jnp.where(s // NT == NF - 1, s % NT, 0), 0)),
                   any_spec, any_spec],
        out_shape=[jax.ShapeDtypeStruct((NF, TOK, 2 * FT), BF16), jax.ShapeDtypeStruct((TOK, D), BF16),
                   jax.ShapeDtypeStruct((UNITS, D, 2 * FT), BF16), jax.ShapeDtypeStruct((UNITS, FT, D), BF16)],
        scratch_shapes=[pltpu.VMEM((TOK, D), BF16), pltpu.VMEM((TOK, D), F32),
                        pltpu.VMEM((UNITS, D, 2 * FT), BF16), pltpu.VMEM((UNITS, FT, D), BF16),
                        pltpu.SemaphoreType.DMA((UNITS, 2)), pltpu.SemaphoreType.DMA((UNITS, 5, 2)),
                        pltpu.SemaphoreType.DMA((UNITS, 5, 2)), pltpu.SemaphoreType.DMA((UNITS, 2))],
        compiler_params=pltpu.CompilerParams(collective_id=1, has_side_effects=True, vmem_limit_bytes=VMEM_MAX),
        cost_estimate=pl.CostEstimate(flops=6 * TOK * D * FF, bytes_accessed=100 << 20, transcendentals=0),
        name="forward_gather",
    )(x, gain, wg_sh, wu_sh, wd_sh)


def grads_kernel(h1_blk, x_blk, gain_blk, wgu_blk, wd_blk, gu_blk, dy_hbm, prod_out, parts, fin, gain_out,
                 n_all, cot_all, dn_all, acc_gu, acc_d, gain_acc, own, r_core, sum_c, r_x, sum_x, r_y, sum_y, r_z, done,
                 g_recv, g_zrecv, cot_sem, part_sem, own_sem, core_send, core_recv, x_send, x_recv, y_send, y_recv,
                 z_send, z_recv, dz_send, dz_recv, dy_send, dy_recv, fin_sem, gs_send, gs_recv, gz_send, gz_recv):
    step = pl.program_id(0)
    wide = step // NT
    tok = step % NT
    layer0 = step >= NF * NT
    tile = wide % NF
    slot = wide % 2
    shard, xx, cc, yy, zz = place()
    core_dev = {"fsdp": 2 * xx + (1 - cc)}
    x_dev = {"fsdp": 2 * (1 - xx) + cc}
    y_dev = {"replica": 1 - yy}
    z_devs = [{"dp": (zz + k) % 4} for k in (1, 2, 3)]

    def remote(src, dst, send, recv, dev):
        return pltpu.make_async_remote_copy(src_ref=src, dst_ref=dst, send_sem=send, recv_sem=recv, device_id=dev,
                                            device_id_type=MESH_ID)

    half_mine = rows_of(yy * 192, 192, 192)
    half_other = rows_of((1 - yy) * 192, 192, 192)

    def core_copy(j):
        return remote(parts.at[j, 1 - cc], r_core.at[j % 2], core_send, core_recv.at[j % 2], core_dev)

    def own_copy(j):
        return pltpu.make_async_copy(parts.at[j, cc], own, own_sem)

    def x_copy(j):
        return remote(sum_c.at[j % 2, 1 - xx], r_x.at[j % 4], x_send.at[j % 2], x_recv.at[j % 4], x_dev)

    def y_copy(j):
        return remote(sum_x.at[half_other, :], r_y.at[j % 2], y_send, y_recv.at[j % 2], y_dev)

    def z_copies(j):
        return [remote(sum_y.at[rows_of(((zz + k + 1) % 4) * 48, 48, 48), :], r_z.at[j % 2, k], z_send.at[k],
                       z_recv.at[j % 2, k], dev) for k, dev in enumerate(z_devs)]

    def quarter(q):
        return rows_of(yy * 192 + q * 48, 48, 48)

    def done_z_copies(j):
        ref = done.at[j % 4, quarter(zz), :]
        return [remote(ref, ref, dz_send.at[k], dz_recv.at[j % 2, k], dev) for k, dev in enumerate(z_devs)]

    def done_y_copy(j):
        ref = done.at[j % 4, half_mine, :]
        return remote(ref, ref, dy_send, dy_recv.at[j % 2], y_dev)

    def fin_copy(j):
        return pltpu.make_async_copy(done.at[j % 4], fin.at[j], fin_sem.at[j % 2])

    def stage0(j):
        whole = parts.at[j]
        pltpu.make_async_copy(whole, whole, part_sem.at[j % 3]).wait()
        own_copy(j).start()
        core_copy(j).start()

    def stage1(j):
        own_copy(j).wait()
        core_copy(j).wait()
        sum_c[j % 2] = own[...] + r_core[j % 2]
        x_copy(j).start()

    def stage2(j):
        x_copy(j).wait()
        sum_x[...] = sum_c[j % 2, xx] + r_x[j % 4]
        y_copy(j).start()

    def stage3(j):
        y_copy(j).wait()
        sum_y[...] = sum_x[half_mine, :] + r_y[j % 2]
        for copy in z_copies(j):
            copy.start()

    def stage4(j):
        for copy in z_copies(j):
            copy.wait()
        done[j % 4, quarter(zz), :] = (sum_y[rows_of(zz * 48, 48, 48), :] + r_z[j % 2, 0]) + (r_z[j % 2, 1] + r_z[j % 2, 2])
        for copy in done_z_copies(j):
            copy.start()

    def stage5(j):
        for copy in done_z_copies(j):
            copy.wait()
        done_y_copy(j).start()

    def stage6(j):
        done_y_copy(j).wait()
        fin_copy(j).start()

    def stage7(j):
        fin_copy(j).wait()

    def tick(count):
        for offset, stage in ((O7, stage7), (O6, stage6), (O5, stage5), (O4, stage4), (O3, stage3), (O2, stage2),
                              (O1, stage1), (0, stage0)):
            job = count - offset

            @pl.when(jnp.logical_and(job >= 0, job < JOBS))
            def _():
                stage(job)

    def write_parts(which, at):
        for s in range(4):
            for k in range(3):
                pltpu.make_async_copy(acc_d.at[at, pl.ds(s * 128, 128), pl.ds(k * 256, 256)],
                                      parts.at[3 * which, s % 2, s // 2, pl.ds(k * 128, 128), :],
                                      part_sem.at[0]).start()
            for m in range(2):
                for k in range(2):
                    pltpu.make_async_copy(acc_gu.at[at, pl.ds(s * GR, GR), pl.ds(m * FT + k * 256, 256)],
                                          parts.at[3 * which + 1 + m, s % 2, s // 2, pl.ds(k * 192, 192), :],
                                          part_sem.at[1 + m]).start()

    @pl.when(step == 0)
    def _():
        load = pltpu.make_async_copy(dy_hbm, cot_all, cot_sem)
        load.start()
        gain_acc[0] = jnp.zeros_like(gain_acc[0])
        entry_barrier((core_dev, x_dev, y_dev, *z_devs))
        load.wait()

    @pl.when(jnp.logical_and(tok == 0, jnp.logical_and(wide >= 1, wide <= TILES)))
    def _():
        write_parts(wide - 1, (wide - 1) % 2)

    in_main = step < MAIN

    @pl.when(jnp.logical_and(jnp.logical_and(in_main, wide >= 1), tok % 3 == 1))
    def _():
        tick(3 * (wide - 1) + tok // 3)

    rows = rows_of(tok * TM, TM, TM)
    first_tok = tok == 0
    first_tile = tile == 0

    def normed(h_ref, row):
        h = h_ref[...].astype(F32)
        n_all[rows, :] = (h * inv_rms_of(h) * gain_blk[row:row + 1, :]).astype(BF16)

    def backward(gu, prod_ref):
        cot = cot_all[rows, :]
        d_prod = dot_nt(cot, wd_blk[0]).astype(BF16).astype(F32)
        gate = gu[:, :FT].astype(F32)
        up = gu[:, FT:].astype(F32)
        sig = sigmoid(gate)
        silu = gate * sig
        prod = (silu * up).astype(BF16)
        if prod_ref is not None:
            prod_ref[0] = prod
        d_up = (d_prod * silu).astype(BF16)
        d_gate = ((d_prod * up) * (sig + silu * (1.0 - sig))).astype(BF16)
        d_gu = jnp.concatenate([d_gate, d_up], axis=1)
        acc_d[slot] = jnp.where(first_tok, 0.0, acc_d[slot]) + dot_tn(prod, cot)
        acc_gu[slot] = jnp.where(first_tok, 0.0, acc_gu[slot]) + dot_tn(n_all[rows, :], d_gu)
        dn_all[rows, :] = jnp.where(first_tile, 0.0, dn_all[rows, :]) + dot_nt(d_gu, wgu_blk[0])

    def norm_backward(h_ref, row, want_hidden):
        h = h_ref[...].astype(F32)
        inv = inv_rms_of(h)
        dn = dn_all[rows, :].astype(BF16).astype(F32)
        part = jnp.sum(dn * h * inv, axis=0, keepdims=True)
        gain_acc[0, row:row + 1, :] = jnp.where(first_tok, 0.0, gain_acc[0, row:row + 1, :]) + part
        if want_hidden:
            scaled = dn * gain_blk[row:row + 1, :]
            back = inv * scaled - h * (inv * inv * inv) * jnp.mean(scaled * h, axis=-1, keepdims=True)
            cot_all[rows, :] = (cot_all[rows, :].astype(F32) + back).astype(BF16)

    @pl.when(jnp.logical_not(layer0))
    def _():
        @pl.when(first_tile)
        def _():
            normed(h1_blk, 1)

        backward(dot_nn(n_all[rows, :], wgu_blk[0]).astype(BF16), prod_out)

        @pl.when(tile == NF - 1)
        def _():
            norm_backward(h1_blk, 1, True)

    @pl.when(jnp.logical_and(layer0, in_main))
    def _():
        @pl.when(first_tile)
        def _():
            normed(x_blk, 0)

        backward(gu_blk[0], None)

        @pl.when(tile == NF - 1)
        def _():
            norm_backward(x_blk, 0, False)

    def gain_copy(leg, dev):
        return remote(gain_acc.at[leg], g_recv.at[leg], gs_send.at[leg], gs_recv.at[leg], dev)

    def gain_z_copies():
        return [remote(g_zrecv.at[zz], g_zrecv.at[zz], gz_send.at[k], gz_recv.at[k], dev)
                for k, dev in enumerate(z_devs)]

    legs = (core_dev, x_dev, y_dev)

    @pl.when(jnp.logical_not(in_main))
    def _():
        tick(3 * (TILES - 1) + step - MAIN)

        for leg in range(4):
            @pl.when(step == MAIN + 1 + leg)
            def _():
                if leg > 0:
                    gain_copy(leg - 1, legs[leg - 1]).wait()
                    total = gain_acc[leg - 1] + g_recv[leg - 1]
                    if leg < 3:
                        gain_acc[leg] = total
                    else:
                        g_zrecv[zz] = total
                if leg < 3:
                    gain_copy(leg, legs[leg]).start()
                else:
                    for copy in gain_z_copies():
                        copy.start()

        @pl.when(step == MAIN + 6)
        def _():
            for copy in gain_z_copies():
                copy.wait()
            gain_out[...] = (g_zrecv[0] + g_zrecv[1]) + (g_zrecv[2] + g_zrecv[3])


def backward_reduce(h1, x, gain, wgu, wd, gu0, dy):
    any_spec = pl.BlockSpec(memory_space=pl.ANY)
    half = NF * NT

    def hold(s, base):
        r = jnp.clip(s - base, 0, half - 1)
        return (jnp.where(jnp.logical_or(r // NT == 0, r // NT == NF - 1), r % NT, NT - 1), 0)

    def unit_index(s):
        wide = jnp.minimum(s, MAIN - 1) // NT
        return (jnp.where(wide < NF, NF + wide, wide - NF), 0, 0)

    def gu_index(s):
        r = jnp.clip(s - half, 0, half - 1)
        return (r // NT, r % NT, 0)

    def prod_index(s):
        r = jnp.minimum(s, half - 1)
        return (r // NT, r % NT, 0)

    dma = pltpu.SemaphoreType.DMA
    return pl.pallas_call(
        grads_kernel,
        grid=(MAIN + DRAIN,),
        in_specs=[pl.BlockSpec((TM, D), lambda s: hold(s, 0)), pl.BlockSpec((TM, D), lambda s: hold(s, half)),
                  pl.BlockSpec((LAYERS, D), lambda s: (0, 0)), pl.BlockSpec((1, D, 2 * FT), unit_index),
                  pl.BlockSpec((1, FT, D), unit_index), pl.BlockSpec((1, TM, 2 * FT), gu_index), any_spec],
        out_specs=[pl.BlockSpec((1, TM, FT), prod_index), any_spec, any_spec,
                   pl.BlockSpec((8, D), lambda s: (0, 0))],
        out_shape=[jax.ShapeDtypeStruct((NF, TOK, FT), BF16), jax.ShapeDtypeStruct((JOBS, 2, 2, *BLK), F32),
                   jax.ShapeDtypeStruct((JOBS, *BLK), F32), jax.ShapeDtypeStruct((8, D), F32)],
        scratch_shapes=[pltpu.VMEM((TOK, D), BF16), pltpu.VMEM((TOK, D), BF16), pltpu.VMEM((TOK, D), F32),
                        pltpu.VMEM((2, D, 2 * FT), F32), pltpu.VMEM((2, FT, D), F32), pltpu.VMEM((3, 8, D), F32),
                        pltpu.VMEM((2, *BLK), F32), pltpu.VMEM((2, 2, *BLK), F32), pltpu.VMEM((2, 2, *BLK), F32),
                        pltpu.VMEM((4, *BLK), F32), pltpu.VMEM(BLK, F32), pltpu.VMEM((2, 192, 256), F32),
                        pltpu.VMEM((192, 256), F32), pltpu.VMEM((2, 3, 48, 256), F32), pltpu.VMEM((4, *BLK), F32),
                        pltpu.VMEM((3, 8, D), F32), pltpu.VMEM((4, 8, D), F32),
                        dma, dma((3,)), dma, dma, dma((2,)), dma((2,)), dma((4,)), dma, dma((2,)),
                        dma((3,)), dma((2, 3)), dma((3,)), dma((2, 3)), dma, dma((2,)), dma((2,)),
                        dma((3,)), dma((3,)), dma((3,)), dma((3,))],
        compiler_params=pltpu.CompilerParams(collective_id=2, has_side_effects=True, vmem_limit_bytes=VMEM_MAX),
        cost_estimate=pl.CostEstimate(flops=28 * TOK * D * FF, bytes_accessed=300 << 20, transcendentals=0),
        name="backward_reduce",
    )(h1, x, gain, wgu, wd, gu0, dy)


def output_kernel(h1_blk, prod_blk, wd_blk, fin, y_out, d_gate, d_up, d_down, stage, load_sem, store_sem):
    step = pl.program_id(0)

    def fin_load(at, i):
        return pltpu.make_async_copy(fin.at[6 * at + i], stage.at[at % 3, i], load_sem.at[at % 3, i])

    def fin_store(at, i):
        wide = 2 * at + i // 3
        layer = 1 - wide // NF
        col = (wide % NF) * 128
        src = stage.at[at % 3, i]
        sem = store_sem.at[at % 3, i]
        if i % 3 == 0:
            for k in range(3):
                pltpu.make_async_copy(src.at[pl.ds(k * 128, 128), :],
                                      d_down.at[layer, rows_of(col, 128, 128), pl.ds(k * 256, 256)], sem).start()
        else:
            dst = d_gate if i % 3 == 1 else d_up
            for k in range(2):
                for g in range(2):
                    pltpu.make_async_copy(src.at[pl.ds(k * GR, GR), pl.ds(g * 128, 128)],
                                          dst.at[layer, :, rows_of((2 * k + g) * D + col, 128, 128)], sem).start()

    def fin_stored(at, i):
        src = stage.at[at % 3, i]
        pltpu.make_async_copy(src, src, store_sem.at[at % 3, i]).wait()

    per = JOBS // 6

    @pl.when(step >= 2)
    def _():
        for i in range(6):
            fin_stored(step - 2, i)

    @pl.when(jnp.logical_and(step >= 1, step <= per))
    def _():
        for i in range(6):
            fin_load(step - 1, i).wait()
            fin_store(step - 1, i)

    @pl.when(step < per)
    def _():
        for i in range(6):
            fin_load(step, i).start()

    out = dot_nn(prod_blk[0], wd_blk[0])
    for f in range(1, NF):
        out = out + dot_nn(prod_blk[f], wd_blk[f])
    y_out[...] = (h1_blk[...].astype(F32) + out).astype(BF16)


def layer_output(h1, prod, wd, fin):
    any_spec = pl.BlockSpec(memory_space=pl.ANY)
    shard = jax.ShapeDtypeStruct((LAYERS, GR, FF), F32)
    return pl.pallas_call(
        output_kernel,
        grid=(NT,),
        in_specs=[pl.BlockSpec((TM, D), lambda t: (t, 0)), pl.BlockSpec((NF, TM, FT), lambda t: (0, t, 0)),
                  pl.BlockSpec((NF, FT, D), lambda t: (1, 0, 0)), any_spec],
        out_specs=[pl.BlockSpec((TM, D), lambda t: (t, 0)), any_spec, any_spec, any_spec],
        out_shape=[jax.ShapeDtypeStruct((TOK, D), BF16), shard, shard, jax.ShapeDtypeStruct((LAYERS, D, D), F32)],
        scratch_shapes=[pltpu.VMEM((3, 6, *BLK), F32), pltpu.SemaphoreType.DMA((3, 6)), pltpu.SemaphoreType.DMA((3, 6))],
        compiler_params=pltpu.CompilerParams(vmem_limit_bytes=VMEM_MAX),
        cost_estimate=pl.CostEstimate(flops=2 * TOK * D * FF, bytes_accessed=72 << 20, transcendentals=0),
        name="layer_output",
    )(h1, prod, wd, fin)


def solution(mesh):
    tok_spec = P(TOKEN_AXES, None)
    shard_spec = P(None, "fsdp", None)
    full_spec = P(None, None)

    def device_step(x_local, dy_local, w_gate_sh, w_up_sh, w_down_sh, norm_gain):
        gu0, h1, wgu, wd = forward_gather(x_local, norm_gain, w_gate_sh, w_up_sh, w_down_sh)
        prod1, _, fin, gain_sum = backward_reduce(h1, x_local, norm_gain, wgu, wd, gu0, dy_local)
        y_local, d_gate, d_up, d_down = layer_output(h1, prod1, wd, fin)
        return y_local, d_gate, d_up, d_down, gain_sum[:LAYERS]

    return jax.shard_map(device_step, mesh=mesh,
                         in_specs=(tok_spec, tok_spec, shard_spec, shard_spec, shard_spec, full_spec),
                         out_specs=(tok_spec, shard_spec, shard_spec, shard_spec, full_spec), check_vma=False)
```

time: 1330 us -> 651 us (0.49)
  waiting for transfers between devices: 659 us -> 0 us
  Pallas kernels: 0 us -> 649 us
  matrix products: 552 us -> 0 us
  blocking collectives: 41.1 us -> 0 us
  local copies, waits for them, and re-layouts: 34.8 us -> 1.33 us
  other arithmetic: 24.8 us -> 0 us
  between operations: 14.6 us -> 0.66 us
    pallas_call x0 -> x3, Pallas kernels: none -> 649 us  [the longest x1 485 us: backward_reduce(): pl.pallas_call(grads_kernel, grid=(MAIN + DRAIN,), in_specs=[pl.BlockSpec...]
    dot_general x18 -> x0, matrix products: 552 us -> none  [the longest x2 86.6 us: layer_forward(): jnp.dot(normed, w_gate, preferred_element_type=jnp.float32)]
    psum x1 -> x0, waiting for transfers between devices: 312 us -> none  [reduce_grad(): return lax.psum(grad_shard, COPY_AXES)]
    reduce_scatter x6 -> x0, waiting for transfers between devices: 289 us -> none  [reduce_grad(): lax.psum_scatter(grad_local, 'fsdp', scatter_dimension=0, tiled=True)]
    all_gather x6 -> x0, waiting for transfers between devices: 55.8 us -> none  [the longest x2 24 us: gather_layer(): up_full = lax.all_gather(w_up_sh[layer_idx], 'fsdp', axis=0, tiled=True)]
    psum x1 -> x0, blocking collectives: 41.1 us -> none  [device_step(): gain_sum = lax.psum(stacked[3], TOKEN_AXES)]
    unnamed x43 -> x0, local copies, waits for them, and re-layouts: 26.1 us -> none
    another operation x3 -> x0, other arithmetic: 13.6 us -> none  [device_step(): jnp.stack([grad_map[layer_idx][part_idx] for layer_idx in range(num_layer...]
  transfers between devices with their start and end apart: 13 -> 0, of which waited for: 10 -> 0; matrix products, arithmetic and copies ran while one was open for 39% -> 0% of each run, Pallas kernels for 0% -> 0%
where the time goes in v1:
time: 651 us
  Pallas kernels  649 us (100%)
    pallas_call x1, Pallas kernels, backward_reduce(): pl.pallas_call(grads_kernel, grid=(MAIN + DRAIN,), in_specs=[pl.BlockSpec...  485 us
    pallas_call x1, Pallas kernels, forward_gather(): pl.pallas_call(gather_kernel, grid=(NF * NT,), in_specs=[pl.BlockSpec((TM...  128 us
    pallas_call x1, Pallas kernels, layer_output(): pl.pallas_call(output_kernel, grid=(NT,), in_specs=[pl.BlockSpec((TM, D),...  36.3 us

profile of v1, /device:TPU:0, one launch (start us, length us, event | category | flops | bytes accessed | tf_op | source)
XLA Modules:
  0.0 651.2 jit_solution(17547093540634934822)
XLA Ops:
  0.6 128.0 %forward_gather.1 = (bf16[6,4096,1024]{2,1,0:T(8,128)(2,1)}, bf16[4096,768]{1,0:T(8,128)(2,1)}, bf16[12,768,1024]{2,1,0:T(8,128)(2,1)}, bf16[12,512,768]{2,1,0:T(8,128)(2,1)}) custom-call(bf16[4096,768]{1,0:T(8,128)(2,1)} %x_blk.3, f32[2,768]{1,0:T(2,128)} %gain_blk.3, bf16[2,192,3072]{2,1,0:T(8,128)(2,1)} %wg_sh.1, bf16[2,192,3072]{2,1,0:T(8,128)(2,1)} %wu_sh.1, ...), custom_call_target="tpu_custom_call" | custom-call | flops 57982058496 | bytes 104857600 | tf_op jit(solution)/shard_map/forward_gather/pallas_call | solution.py:216
  128.6 484.9 %backward_reduce.1 = (bf16[6,4096,512]{2,1,0:T(8,128)(2,1)}, f32[36,2,2,384,256]{4,3,2,1,0:T(8,128)}, f32[36,384,256]{2,1,0:T(8,128)}, f32[8,768]{1,0:T(8,128)}) custom-call(bf16[4096,768]{1,0:T(8,128)(2,1)} %get-tuple-element.16.h1_blk, bf16[4096,768]{1,0:T(8,128)(2,1)} %x_blk.3, f32[2,768]{1,0:T(2,128)} %gain_blk.3, ...), custom_call_target="tpu_custom_call" | custom-call | flops 270582939648 | bytes 314572800 | tf_op jit(solution)/shard_map/backward_reduce/pallas_call | solution.py:487
  613.5 36.3 %layer_output.1 = (bf16[4096,768]{1,0:T(8,128)(2,1)}, f32[2,192,3072]{2,1,0:T(8,128)}, f32[2,192,3072]{2,1,0:T(8,128)}, f32[2,768,768]{2,1,0:T(8,128)}) custom-call(bf16[4096,768]{1,0:T(8,128)(2,1)} %get-tuple-element.16.h1_blk, bf16[6,4096,512]{2,1,0:T(8,128)(2,1)} %get-tuple-element.20.prod_blk, bf16[12,512,768]{2,1,0:T(8,128)(2,1)} %get-tuple-element.18.wd_blk, ...), custom_call_target="tpu_custom_call" | custom-call | flops 19327352832 | bytes 75497472 | tf_op jit(solution)/shard_map/layer_output/pallas_call | solution.py:566
  649.8 1.3 slice.3

commit v2 on v1

v2 whole, which is shorter than its diff:
```python
import jax
import jax.numpy as jnp
from jax import lax
from jax.experimental import pallas as pl
from jax.experimental.pallas import tpu as pltpu
from jax.sharding import PartitionSpec as P

NORM_EPS = 1e-6
TOKEN_AXES = ("dp", "replica", "fsdp")
MESH_ID = pl.DeviceIdType.MESH
BF16 = jnp.bfloat16
F32 = jnp.float32

TOK = 4096
D = 768
FF = 3072
LAYERS = 2
TM = 512
NT = TOK // TM
FT = 512
NF = FF // FT
GR = D // 4
UNITS = LAYERS * NF
TILES = LAYERS * NF
JOBS = 3 * TILES
BLK = (384, 256)
VMEM_MAX = 67043328
O1, O2, O3, O4, O5, O6, O7 = 1, 4, 6, 9, 13, 17, 18
BEATS = 2 * (JOBS - 1) + O7 + 1
MAIN = LAYERS * NF * NT
STEPS = MAIN + NF * NT
AHEAD = 6
SLOW = 36


def dot_nn(a, b):
    return lax.dot_general(a, b, (((1,), (0,)), ((), ())), preferred_element_type=F32)


def dot_nt(a, b):
    return lax.dot_general(a, b, (((1,), (1,)), ((), ())), preferred_element_type=F32)


def dot_tn(a, b):
    return lax.dot_general(a, b, (((0,), (0,)), ((), ())), preferred_element_type=F32)


def sigmoid(v):
    return 0.5 * jnp.tanh(0.5 * v) + 0.5


def inv_rms_of(h):
    return lax.rsqrt(jnp.mean(h * h, axis=-1, keepdims=True) + NORM_EPS)


def rows_of(start, size):
    return pl.ds(pl.multiple_of(start, size), size)


def place():
    shard = lax.axis_index("fsdp")
    return shard, shard // 2, shard % 2, lax.axis_index("replica"), lax.axis_index("dp")


def signal_entry(partners):
    for partner in partners:
        pl.semaphore_signal(pltpu.get_barrier_semaphore(), inc=1, device_id=partner, device_id_type=MESH_ID)


def wait_entry(partners):
    pl.semaphore_wait(pltpu.get_barrier_semaphore(), len(partners))


def gather_kernel(x_hbm, gain_hbm, wg_sh, wu_sh, wd_sh, gu_hbm, h1_hbm, wgu_hbm, wd_hbm,
                  n_all, acc, prods, wgu, wd, x_buf, gu_buf, h1_buf, gain, load_sem, send_sem, recv_sem, out_sem,
                  x_sem, gu_sem, h1_sem, in_sem):
    step = pl.program_id(0)
    last = NF * NT - 1
    tile = jnp.minimum(step, last) >> 3
    tok = step & 7
    prev = jnp.maximum(step - 1, 0)
    prev_tile = prev >> 3
    side = step & 1
    shard, xx, cc, yy, zz = place()
    core_dev = {"fsdp": 2 * xx + (1 - cc)}
    x_dev = {"fsdp": 2 * (1 - xx) + cc}
    y_dev = {"replica": 1 - yy}
    core_sh = 2 * xx + (1 - cc)
    x_sh = 2 * (1 - xx) + cc
    far_sh = 2 * (1 - xx) + (1 - cc)
    both = (0, 1)

    def part(unit, owner, half):
        if half is None:
            return wgu.at[unit, rows_of(owner * GR, GR), :], wd.at[unit, rows_of(owner * 128, 128), :]
        return (wgu.at[unit, rows_of(owner * GR + half * 96, 96), :],
                wd.at[unit, rows_of(owner * 128 + half * 64, 64), :])

    def message(unit, kind, owner, half, dev, which=both):
        refs = part(unit, owner, half)
        return [pltpu.make_async_remote_copy(src_ref=refs[i], dst_ref=refs[i], send_sem=send_sem.at[kind, i],
                                             recv_sem=recv_sem.at[unit, kind, i], device_id=dev,
                                             device_id_type=MESH_ID)
                for i in which]

    def send(*args):
        for copy in message(*args):
            copy.start()

    def arrived(*args):
        for copy in message(*args):
            copy.wait_recv()

    def load(unit):
        layer = lax.div(unit, NF)
        col = lax.rem(unit, NF) * 128
        for group in range(4):
            cols = rows_of(group * D + col, 128)
            pltpu.make_async_copy(wg_sh.at[layer, :, cols],
                                  wgu.at[unit, rows_of(shard * GR, GR), pl.ds(group * 128, 128)],
                                  load_sem.at[unit, 0]).start()
            pltpu.make_async_copy(wu_sh.at[layer, :, cols],
                                  wgu.at[unit, rows_of(shard * GR, GR), pl.ds(FT + group * 128, 128)],
                                  load_sem.at[unit, 0]).start()
        pltpu.make_async_copy(wd_sh.at[layer, rows_of(col, 128), :],
                              wd.at[unit, rows_of(shard * 128, 128), :], load_sem.at[unit, 1]).start()

    def send_own(unit):
        own = part(unit, shard, None)
        for i in both:
            pltpu.make_async_copy(own[i], own[i], load_sem.at[unit, i]).wait()
            send(unit, 1, shard, yy, x_dev, (i,))
            send(unit, 0, shard, None, core_dev, (i,))

    def forward_x(unit, which=both):
        for i in which:
            arrived(unit, 1, x_sh, yy, x_dev, (i,))
            send(unit, 2, x_sh, yy, y_dev, (i,))
            send(unit, 3, x_sh, yy, core_dev, (i,))

    def forward_y(unit, which=both):
        for i in which:
            arrived(unit, 2, x_sh, 1 - yy, y_dev, (i,))
            send(unit, 4, x_sh, 1 - yy, core_dev, (i,))

    def out_copy(unit, i):
        if i == 0:
            return pltpu.make_async_copy(wgu.at[unit], wgu_hbm.at[unit], out_sem.at[0])
        return pltpu.make_async_copy(wd.at[unit], wd_hbm.at[unit], out_sem.at[1])

    def complete(unit, which=both):
        for i in which:
            arrived(unit, 0, core_sh, None, core_dev, (i,))
            arrived(unit, 3, far_sh, yy, core_dev, (i,))
            arrived(unit, 4, far_sh, 1 - yy, core_dev, (i,))
            out_copy(unit, i).start()

    def token_rows(at):
        return rows_of((at & 7) * TM, TM)

    def x_copy(at):
        return pltpu.make_async_copy(x_hbm.at[token_rows(at - 1), :], x_buf.at[at & 1], x_sem.at[at & 1])

    def gu_copy(at):
        return pltpu.make_async_copy(gu_buf.at[at & 1], gu_hbm.at[at >> 3, token_rows(at), :], gu_sem.at[at & 1])

    def h1_copy(at):
        return pltpu.make_async_copy(h1_buf.at[at & 1], h1_hbm.at[token_rows(at - 1), :], h1_sem.at[at & 1])

    @pl.when(step == 0)
    def _():
        signal_entry((core_dev, x_dev, y_dev))
        pltpu.make_async_copy(x_hbm, n_all, in_sem.at[0]).start()
        pltpu.make_async_copy(gain_hbm, gain, in_sem.at[1]).start()

        @pl.loop(0, UNITS)
        def _(unit):
            load(unit)

        wait_entry((core_dev, x_dev, y_dev))

        @pl.loop(0, 5)
        def _(unit):
            send_own(unit)

        pltpu.make_async_copy(x_hbm, n_all, in_sem.at[0]).wait()
        pltpu.make_async_copy(gain_hbm, gain, in_sem.at[1]).wait()

        @pl.loop(0, NT)
        def _(t):
            rows_t = rows_of(t * TM, TM)
            h = n_all[rows_t, :].astype(F32)
            n_all[rows_t, :] = (h * inv_rms_of(h) * gain[0:1, :]).astype(BF16)

        forward_x(0)
        forward_y(0)
        complete(0)

    @pl.when(jnp.logical_and(step & 3 == 1, (step >> 2) + 1 < UNITS))
    def _():
        unit = (step >> 2) + 1

        @pl.when(unit + 4 < UNITS)
        def _():
            send_own(unit + 4)

        forward_x(unit)

    @pl.when(jnp.logical_and(step & 3 == 2, jnp.logical_and(step >= 4, step >> 2 < UNITS)))
    def _():
        forward_y(step >> 2)

    @pl.when(jnp.logical_and(tok == 0, jnp.logical_and(step > 0, step <= last)))
    def _():
        complete(tile)

    @pl.when(jnp.logical_and(step & 3 == 3, step >> 2 >= NF))
    def _():
        complete(step >> 2)

    @pl.when(jnp.logical_and(step >= last + 1 - NT, step <= last))
    def _():
        x_copy(step + 1).start()

    @pl.when(step >= 2)
    def _():
        gu_copy(step - 2).wait()

    rows = rows_of(tok * TM, TM)
    prev_rows = rows_of((prev & 7) * TM, TM)

    gu = dot_nn(n_all[rows, :], wgu[tile]).astype(BF16)
    acc[prev_rows, :] = jnp.where(prev_tile == 0, 0.0, acc[prev_rows, :]) + dot_nn(prods[1 - side], wd[prev_tile])
    gu_buf[side] = gu
    gate = gu[:, :FT].astype(F32)
    prods[side] = (gate * sigmoid(gate) * gu[:, FT:].astype(F32)).astype(BF16)

    @pl.when(step <= last)
    def _():
        gu_copy(step).start()

    @pl.when(step > last + 1 - NT)
    def _():
        x_copy(step).wait()

        @pl.when(step > last + 3 - NT)
        def _():
            h1_copy(step - 2).wait()

        h1_buf[side] = (x_buf[side].astype(F32) + acc[prev_rows, :]).astype(BF16)
        h1_copy(step).start()

    @pl.when(step == last + 1)
    def _():
        gu_copy(last).wait()
        for at in (last, last + 1):
            h1_copy(at).wait()

        for kind in range(5):
            for i, ref in enumerate((wgu, wd)):
                size = (GR, 128)[i] // (1 if kind == 0 else 2)
                sent = ref.at[:, pl.ds(0, size), :]
                pltpu.make_async_copy(sent, sent, send_sem.at[kind, i]).wait()
        pltpu.make_async_copy(wgu, wgu_hbm, out_sem.at[0]).wait()
        pltpu.make_async_copy(wd, wd_hbm, out_sem.at[1]).wait()


def forward_gather(x, gain, wg_sh, wu_sh, wd_sh):
    any_spec = pl.BlockSpec(memory_space=pl.ANY)
    dma = pltpu.SemaphoreType.DMA
    pair = dma((2,))
    return pl.pallas_call(
        gather_kernel,
        grid=(NF * NT + 1,),
        in_specs=[any_spec] * 5,
        out_specs=[any_spec] * 4,
        out_shape=[jax.ShapeDtypeStruct((NF, TOK, 2 * FT), BF16), jax.ShapeDtypeStruct((TOK, D), BF16),
                   jax.ShapeDtypeStruct((UNITS, D, 2 * FT), BF16), jax.ShapeDtypeStruct((UNITS, FT, D), BF16)],
        scratch_shapes=[pltpu.VMEM((TOK, D), BF16), pltpu.VMEM((TOK, D), F32), pltpu.VMEM((2, TM, FT), BF16),
                        pltpu.VMEM((UNITS, D, 2 * FT), BF16), pltpu.VMEM((UNITS, FT, D), BF16),
                        pltpu.VMEM((2, TM, D), BF16), pltpu.VMEM((2, TM, 2 * FT), BF16), pltpu.VMEM((2, TM, D), BF16),
                        pltpu.VMEM((LAYERS, D), F32),
                        dma((UNITS, 2)), dma((5, 2)), dma((UNITS, 5, 2)), dma((2,)),
                        pair, pair, pair, pair],
        compiler_params=pltpu.CompilerParams(collective_id=1, has_side_effects=True, vmem_limit_bytes=VMEM_MAX),
        cost_estimate=pl.CostEstimate(flops=6 * TOK * D * FF, bytes_accessed=100 << 20, transcendentals=0),
        name="forward_gather",
    )(x, gain, wg_sh, wu_sh, wd_sh)


def grads_kernel(h1_hbm, x_hbm, gain_hbm, wgu_hbm, wd_hbm, gu_hbm, dy_hbm, y_hbm, prod_hbm, parts, fin, gain_sum_hbm,
                 n_all, cot_all, dn_all, acc_gu, acc_d, prod_buf, wgu, wd, h_buf, gu_buf, gain, gain_out,
                 gain_acc, own, r_core, sum_c, r_x, sum_x, r_y, sum_y, r_z, done, g_recv, g_zrecv,
                 in_sem, dy_sem, wgu_sem, wd_sem, h_sem, gu_sem, y_sem, prod_sem, ring_sem, part_sem,
                 own_sem, core_send, core_recv, x_send, x_recv, y_send, y_recv,
                 z_send, z_recv, dz_send, dz_recv, dy_send, dy_recv, fin_sem, gs_send, gs_recv, gz_send, gz_recv):
    step = pl.program_id(0)
    wide = step >> 3
    tok = step & 7
    side = step & 1
    slot = wide & 1
    in_l1 = wide < NF
    in_main = wide < TILES
    in_l0 = jnp.logical_and(wide >= NF, in_main)
    first_tile = wide == TILES
    last_tile = wide == TILES + NF - 1
    reads_h = (wide == 0) | (wide == NF - 1) | (wide == NF) | (wide == TILES)
    shard, xx, cc, yy, zz = place()
    core_dev = {"fsdp": 2 * xx + (1 - cc)}
    x_dev = {"fsdp": 2 * (1 - xx) + cc}
    y_dev = {"replica": 1 - yy}
    z_devs = [{"dp": (zz + k) % 4} for k in (1, 2, 3)]

    def remote(src, dst, send, recv, dev):
        return pltpu.make_async_remote_copy(src_ref=src, dst_ref=dst, send_sem=send, recv_sem=recv, device_id=dev,
                                            device_id_type=MESH_ID)

    half_mine = rows_of(yy * 192, 192)
    half_other = rows_of((1 - yy) * 192, 192)

    def core_copy(j):
        return remote(parts.at[j, 1 - cc], r_core.at[j & 1], core_send, core_recv.at[j & 1], core_dev)

    def own_copy(j):
        return pltpu.make_async_copy(parts.at[j, cc], own, own_sem)

    def x_copy(j):
        return remote(sum_c.at[j & 1, 1 - xx], r_x.at[j & 3], x_send.at[j & 1], x_recv.at[j & 3], x_dev)

    def y_copy(j):
        return remote(sum_x.at[j & 1, half_other, :], r_y.at[j & 3], y_send.at[j & 1], y_recv.at[j & 3], y_dev)

    def z_copies(j):
        return [remote(sum_y.at[j & 1, rows_of(((zz + k + 1) % 4) * 48, 48), :], r_z.at[j & 3, k],
                       z_send.at[j & 1, k], z_recv.at[j & 3, k], dev) for k, dev in enumerate(z_devs)]

    def quarter(q):
        return rows_of(yy * 192 + q * 48, 48)

    def done_z_copies(j):
        ref = done.at[j & 7, quarter(zz), :]
        return [remote(ref, ref, dz_send.at[j & 1, k], dz_recv.at[j & 3, k], dev) for k, dev in enumerate(z_devs)]

    def done_y_copy(j):
        ref = done.at[j & 7, half_mine, :]
        return remote(ref, ref, dy_send.at[j & 1], dy_recv.at[j & 3], y_dev)

    def fin_copy(j):
        return pltpu.make_async_copy(done.at[j & 7], fin.at[j], fin_sem.at[j & 1])

    def stage0(j):
        whole = parts.at[j]
        pltpu.make_async_copy(whole, whole, part_sem.at[lax.rem(j, 3)]).wait()
        own_copy(j).start()
        core_copy(j).start()

    def stage1(j):
        own_copy(j).wait()
        core_copy(j).wait()
        sum_c[j & 1] = own[...] + r_core[j & 1]
        x_copy(j).start()

    def stage2(j):
        x_copy(j).wait()
        sum_x[j & 1] = sum_c[j & 1, xx] + r_x[j & 3]
        y_copy(j).start()

    def stage3(j):
        y_copy(j).wait()
        sum_y[j & 1] = sum_x[j & 1, half_mine, :] + r_y[j & 3]
        for copy in z_copies(j):
            copy.start()

    def stage4(j):
        for copy in z_copies(j):
            copy.wait()
        done[j & 7, quarter(zz), :] = ((sum_y[j & 1, rows_of(zz * 48, 48), :] + r_z[j & 3, 0])
                                       + (r_z[j & 3, 1] + r_z[j & 3, 2]))
        for copy in done_z_copies(j):
            copy.start()

    def stage5(j):
        for copy in done_z_copies(j):
            copy.wait()
        done_y_copy(j).start()

    def stage6(j):
        done_y_copy(j).wait()
        fin_copy(j).start()

    def stage7(j):
        fin_copy(j).wait()

    even_stages = ((O7, stage7), (O3, stage3), (O2, stage2), (0, stage0))
    odd_stages = ((O6, stage6), (O5, stage5), (O4, stage4), (O1, stage1))

    def run_beat(count, parity):
        for offset, stage in (even_stages, odd_stages)[parity]:
            job = (count - offset) >> 1

            @pl.when(jnp.logical_and(count >= offset, job < JOBS))
            def _():
                stage(job)

    def write_parts(which, at):
        for s in range(4):
            for k in range(3):
                pltpu.make_async_copy(acc_d.at[at, pl.ds(s * 128, 128), pl.ds(k * 256, 256)],
                                      parts.at[3 * which, s % 2, s // 2, pl.ds(k * 128, 128), :],
                                      part_sem.at[0]).start()
            for m in range(2):
                for k in range(2):
                    pltpu.make_async_copy(acc_gu.at[at, pl.ds(s * GR, GR), pl.ds(m * FT + k * 256, 256)],
                                          parts.at[3 * which + 1 + m, s % 2, s // 2, pl.ds(k * 192, 192), :],
                                          part_sem.at[1 + m]).start()

    def unit_of(at):
        return jnp.where(at < NF, at + NF, at - NF)

    def wgu_copy(at):
        return pltpu.make_async_copy(wgu_hbm.at[unit_of(at)], wgu.at[at & 1], wgu_sem.at[at & 1])

    def wd_copy(at):
        return pltpu.make_async_copy(wd_hbm.at[unit_of(at)], wd.at[at & 1], wd_sem.at[at & 1])

    def token_rows(at):
        return rows_of((at & 7) * TM, TM)

    def h_copy(at, source):
        return pltpu.make_async_copy(source.at[token_rows(at), :], h_buf.at[at & 1], h_sem.at[at & 1])

    def gu_copy(at):
        return pltpu.make_async_copy(gu_hbm.at[(at >> 3) - NF, token_rows(at), :], gu_buf.at[at & 1], gu_sem.at[at & 1])

    def y_copy_out(at):
        return pltpu.make_async_copy(n_all.at[token_rows(at), :], y_hbm.at[token_rows(at), :], y_sem.at[0])

    def prefetch(at):
        tile = at >> 3
        reads_h1 = jnp.logical_or(tile == 0, tile == NF - 1)

        @pl.when(reads_h1)
        def _():
            h_copy(at, h1_hbm).start()

        @pl.when(jnp.logical_or(tile == NF, tile == TILES))
        def _():
            h_copy(at, x_hbm).start()

        @pl.when(jnp.logical_and(tile >= NF, tile < TILES))
        def _():
            gu_copy(at).start()

    def dy_copy(at):
        return pltpu.make_async_copy(dy_hbm.at[token_rows(at), :], cot_all.at[token_rows(at), :], dy_sem.at[at & 7])

    partners = (core_dev, x_dev, y_dev, *z_devs)

    @pl.when(step == 0)
    def _():
        signal_entry(partners)
        wgu_copy(0).start()
        wd_copy(0).start()
        prefetch(step)
        pltpu.make_async_copy(gain_hbm, gain, in_sem.at[1]).start()
        for at in range(NT):
            dy_copy(at).start()
        gain_acc[0] = jnp.zeros_like(gain_acc[0])
        pltpu.make_async_copy(gain_hbm, gain, in_sem.at[1]).wait()

    @pl.when(step == NT)
    def _():
        wait_entry(partners)

    @pl.when(wide == 0)
    def _():
        dy_copy(step).wait()

    @pl.when(tok == 0)
    def _():
        wd_copy(wide).wait()

        @pl.when(in_main)
        def _():
            wgu_copy(wide).wait()

        @pl.when(wide + 1 < TILES + NF)
        def _():
            wd_copy(wide + 1).start()

        @pl.when(wide + 1 < TILES)
        def _():
            wgu_copy(wide + 1).start()

        @pl.when(jnp.logical_and(wide >= 1, wide <= TILES))
        def _():
            write_parts(wide - 1, (wide - 1) & 1)

    @pl.when(step + 1 < STEPS)
    def _():
        prefetch(step + 1)

    @pl.when(reads_h)
    def _():
        h_copy(step, h1_hbm).wait()

    @pl.when(in_l0)
    def _():
        gu_copy(step).wait()

    beat = 6 * (wide - 1) + tok - jnp.where(tok > 4, 2, 1)
    reducing = jnp.logical_and(jnp.logical_and(in_main, wide >= 1), tok & 3 != 0)
    for parity in range(2):
        @pl.when(jnp.logical_and(reducing, beat & 1 == parity))
        def _():
            run_beat(beat, parity)

    rows = rows_of(tok * TM, TM)
    first_tok = tok == 0

    def prod_copy(at):
        return pltpu.make_async_copy(prod_buf.at[at & 1], prod_hbm.at[at >> 3, token_rows(at), :], prod_sem.at[at & 1])

    def ring(at):
        return cot_all.at[token_rows(at), pl.ds(0, FT)]

    def prod_load(at):
        return pltpu.make_async_copy(prod_hbm.at[at >> 3, token_rows(at), :], ring(at), ring_sem.at[at & 7])

    @pl.when(jnp.logical_and(step >= 2, step < NF * NT + 2))
    def _():
        prod_copy(step - 2).wait()

    def add_gain(row, dn, h, inv):
        part = jnp.sum(dn * h * inv, axis=0, keepdims=True)
        gain_acc[0, row:row + 1, :] = jnp.where(first_tok, 0.0, gain_acc[0, row:row + 1, :]) + part

    def backward(layer, first, last):
        cot = cot_all[rows, :]
        gain_row = gain[layer:layer + 1, :]
        if first or last:
            h = h_buf[side].astype(F32)
            inv = inv_rms_of(h)
        if first:
            normed = (h * inv * gain_row).astype(BF16)
            n_all[rows, :] = normed
        else:
            normed = n_all[rows, :]
        gu = dot_nn(normed, wgu[slot]).astype(BF16) if layer else gu_buf[side]
        d_prod = dot_nt(cot, wd[slot]).astype(BF16).astype(F32)
        gate = gu[:, :FT].astype(F32)
        up = gu[:, FT:].astype(F32)
        sig = sigmoid(gate)
        silu = gate * sig
        prod = (silu * up).astype(BF16)
        if layer:
            prod_buf[side] = prod
        d_up = (d_prod * silu).astype(BF16)
        d_gate = ((d_prod * up) * (sig + silu * (1.0 - sig))).astype(BF16)
        d_gu = jnp.concatenate([d_gate, d_up], axis=1)

        def add_weights():
            acc_d[slot] = jnp.where(first_tok, 0.0, acc_d[slot]) + dot_tn(prod, cot)
            acc_gu[slot] = jnp.where(first_tok, 0.0, acc_gu[slot]) + dot_tn(normed, d_gu)

        if not last:
            add_weights()
        dn = dot_nt(d_gu, wgu[slot])
        if not first:
            dn = dn_all[rows, :] + dn
        if last:
            dn = dn.astype(BF16).astype(F32)
            add_gain(layer, dn, h, inv)
            scaled = dn * gain_row
            back = inv * scaled - h * (inv * inv * inv * jnp.mean(scaled * h, axis=-1, keepdims=True))
            cot_all[rows, :] = (cot.astype(F32) + back).astype(BF16)
            add_weights()
        else:
            dn_all[rows, :] = dn

    @pl.when(wide == 0)
    def _():
        backward(1, True, False)

    @pl.when(jnp.logical_and(wide > 0, wide < NF - 1))
    def _():
        backward(1, False, False)

    @pl.when(wide == NF - 1)
    def _():
        backward(1, False, True)

    @pl.when(in_l1)
    def _():
        prod_copy(step).start()

    @pl.when(wide == NF)
    def _():
        backward(0, True, False)

    @pl.when(jnp.logical_and(wide > NF, in_main))
    def _():
        backward(0, False, False)

    @pl.when(wide == TILES)
    def _():
        h = h_buf[side].astype(F32)
        add_gain(0, dn_all[rows, :].astype(BF16).astype(F32), h, inv_rms_of(h))

    def gain_copy(leg, dev):
        return remote(gain_acc.at[leg], g_recv.at[leg], gs_send.at[leg], gs_recv.at[leg], dev)

    def gain_z_copies():
        return [remote(g_zrecv.at[zz], g_zrecv.at[zz], gz_send.at[k], gz_recv.at[k], dev)
                for k, dev in enumerate(z_devs)]

    legs = (core_dev, x_dev, y_dev)
    rest = step - MAIN

    h1_load = pltpu.make_async_copy(h1_hbm, n_all, y_sem.at[1])

    @pl.when(rest == 0)
    def _():
        for at in range(AHEAD):
            prod_load(at).start()
        h1_load.start()

    @pl.when(rest >= 0)
    def _():
        full = rest < SLOW
        late = 6 * (TILES - 1) + jnp.where(full, lax.div(rest, 3), rest - SLOW + SLOW // 3)
        due = jnp.logical_or(jnp.logical_not(full), lax.rem(rest, 3) == 0)

        @pl.when(rest + AHEAD < NF * NT)
        def _():
            prod_load(rest + AHEAD).start()

        for parity in range(2):
            @pl.when(jnp.logical_and(due, jnp.logical_and(late & 1 == parity, late < BEATS)))
            def _():
                run_beat(late, parity)

        for leg, at in enumerate((9, 13, 27, 35)):
            @pl.when(rest == at)
            def _():
                if leg > 0:
                    gain_copy(leg - 1, legs[leg - 1]).wait()
                    total = gain_acc[leg - 1] + g_recv[leg - 1]
                    if leg < 3:
                        gain_acc[leg] = total
                    else:
                        g_zrecv[zz] = total
                if leg < 3:
                    gain_copy(leg, legs[leg]).start()
                else:
                    for copy in gain_z_copies():
                        copy.start()

        @pl.when(rest == 45)
        def _():
            for copy in gain_z_copies():
                copy.wait()
            gain_out[...] = ((g_zrecv[0] + g_zrecv[1]) + (g_zrecv[2] + g_zrecv[3]))[:LAYERS]
            pltpu.make_async_copy(gain_out, gain_sum_hbm, in_sem.at[1]).start()

        prod_load(rest).wait()
        dn_all[rows, :] = jnp.where(first_tile, 0.0, dn_all[rows, :]) + dot_nn(ring(rest)[...], wd[slot])

        @pl.when(last_tile)
        def _():
            @pl.when(first_tok)
            def _():
                h1_load.wait()

            n_all[rows, :] = (n_all[rows, :].astype(F32) + dn_all[rows, :]).astype(BF16)
            y_copy_out(step).start()

        @pl.when(step == STEPS - 1)
        def _():
            pltpu.make_async_copy(gain_out, gain_sum_hbm, in_sem.at[1]).wait()
            pltpu.make_async_copy(n_all, y_hbm, y_sem.at[0]).wait()


def backward_reduce(h1, x, gain, wgu, wd, gu0, dy):
    any_spec = pl.BlockSpec(memory_space=pl.ANY)
    dma = pltpu.SemaphoreType.DMA
    pair, trio, quad, ring = (dma((n,)) for n in (2, 3, 4, 8))
    two_blk = pltpu.VMEM((2, *BLK), F32)
    z_sems = (dma((2, 3)), dma((4, 3)))
    return pl.pallas_call(
        grads_kernel,
        grid=(STEPS,),
        in_specs=[any_spec] * 7,
        out_specs=[any_spec] * 5,
        out_shape=[jax.ShapeDtypeStruct((TOK, D), BF16), jax.ShapeDtypeStruct((NF, TOK, FT), BF16),
                   jax.ShapeDtypeStruct((JOBS, 2, 2, *BLK), F32), jax.ShapeDtypeStruct((JOBS, *BLK), F32),
                   jax.ShapeDtypeStruct((LAYERS, D), F32)],
        scratch_shapes=[pltpu.VMEM((TOK, D), BF16), pltpu.VMEM((TOK, D), BF16), pltpu.VMEM((TOK, D), F32),
                        pltpu.VMEM((2, D, 2 * FT), F32), pltpu.VMEM((2, FT, D), F32), pltpu.VMEM((2, TM, FT), BF16),
                        pltpu.VMEM((2, D, 2 * FT), BF16), pltpu.VMEM((2, FT, D), BF16), pltpu.VMEM((2, TM, D), BF16),
                        pltpu.VMEM((2, TM, 2 * FT), BF16), pltpu.VMEM((LAYERS, D), F32),
                        pltpu.VMEM((LAYERS, D), F32), pltpu.VMEM((3, 8, D), F32),
                        two_blk, pltpu.VMEM((2, 2, *BLK), F32), pltpu.VMEM((2, 2, *BLK), F32),
                        pltpu.VMEM((4, *BLK), F32), two_blk, pltpu.VMEM((4, 192, 256), F32),
                        pltpu.VMEM((2, 192, 256), F32), pltpu.VMEM((4, 3, 48, 256), F32), pltpu.VMEM((8, *BLK), F32),
                        pltpu.VMEM((3, 8, D), F32), pltpu.VMEM((4, 8, D), F32),
                        pair, ring, pair, pair, pair, pair, pair, pair, ring, trio,
                        dma, dma, pair, pair, quad, pair, quad, *z_sems, *z_sems, pair, quad, pair, trio, trio, trio, trio],
        compiler_params=pltpu.CompilerParams(collective_id=2, has_side_effects=True, vmem_limit_bytes=VMEM_MAX),
        cost_estimate=pl.CostEstimate(flops=30 * TOK * D * FF, bytes_accessed=320 << 20, transcendentals=0),
        name="backward_reduce",
    )(h1, x, gain, wgu, wd, gu0, dy)


def place_kernel(fin, y_in, gain_in, d_gate, d_up, d_down, y_out, gain_out, stage, y_stage, load_sem, store_sem, y_load, y_store):
    def fin_load(job):
        return pltpu.make_async_copy(fin.at[job], stage.at[job], load_sem.at[job])

    def fin_store(job):
        layer = 1 - job // (3 * NF)
        col = (job // 3 % NF) * 128
        src = stage.at[job]
        sem = store_sem.at[job]
        if job % 3 == 0:
            for k in range(3):
                pltpu.make_async_copy(src.at[pl.ds(k * 128, 128), :],
                                      d_down.at[layer, pl.ds(col, 128), pl.ds(k * 256, 256)], sem).start()
        else:
            dst = d_gate if job % 3 == 1 else d_up
            for k in range(2):
                for g in range(2):
                    pltpu.make_async_copy(src.at[pl.ds(k * GR, GR), pl.ds(g * 128, 128)],
                                          dst.at[layer, :, pl.ds((2 * k + g) * D + col, 128)], sem).start()

    def y_copies(t):
        rows = pl.ds(t * TM, TM)
        return (pltpu.make_async_copy(y_in.at[rows, :], y_stage.at[rows, :], y_load.at[t]),
                pltpu.make_async_copy(y_stage.at[rows, :], y_out.at[rows, :], y_store.at[t]))

    gain_out[...] = gain_in[...]
    for t in range(NT):
        y_copies(t)[0].start()
    for job in range(JOBS):
        fin_load(job).start()
    for t in range(NT):
        load, store = y_copies(t)
        load.wait()
        store.start()
    for job in range(JOBS):
        fin_load(job).wait()
        fin_store(job)
    for t in range(NT):
        y_copies(t)[1].wait()
    for job in range(JOBS):
        src = stage.at[job]
        pltpu.make_async_copy(src, src, store_sem.at[job]).wait()


def place_grads(fin, y, gain_sum):
    any_spec = pl.BlockSpec(memory_space=pl.ANY)
    shard = jax.ShapeDtypeStruct((LAYERS, GR, FF), F32)
    dma = pltpu.SemaphoreType.DMA
    return pl.pallas_call(
        place_kernel,
        in_specs=[any_spec, any_spec, pl.BlockSpec(memory_space=pltpu.VMEM)],
        out_specs=[*[any_spec] * 4, pl.BlockSpec(memory_space=pltpu.VMEM)],
        out_shape=[shard, shard, jax.ShapeDtypeStruct((LAYERS, D, D), F32), jax.ShapeDtypeStruct((TOK, D), BF16),
                   jax.ShapeDtypeStruct((LAYERS, D), F32)],
        scratch_shapes=[pltpu.VMEM((JOBS, *BLK), F32), pltpu.VMEM((TOK, D), BF16), dma((JOBS,)), dma((JOBS,)),
                        dma((NT,)), dma((NT,))],
        compiler_params=pltpu.CompilerParams(vmem_limit_bytes=VMEM_MAX),
        cost_estimate=pl.CostEstimate(flops=0, bytes_accessed=41 << 20, transcendentals=0),
        name="place_grads",
    )(fin, y, gain_sum)


def solution(mesh):
    tok_spec = P(TOKEN_AXES, None)
    shard_spec = P(None, "fsdp", None)
    full_spec = P(None, None)

    def device_step(x_local, dy_local, w_gate_sh, w_up_sh, w_down_sh, norm_gain):
        gu0, h1, wgu, wd = forward_gather(x_local, norm_gain, w_gate_sh, w_up_sh, w_down_sh)
        y_local, _, _, fin, gain_sum = backward_reduce(h1, x_local, norm_gain, wgu, wd, gu0, dy_local)
        d_gate, d_up, d_down, y_out, d_gain = place_grads(fin, y_local, gain_sum)
        return y_out, d_gate, d_up, d_down, d_gain

    return jax.shard_map(device_step, mesh=mesh,
                         in_specs=(tok_spec, tok_spec, shard_spec, shard_spec, shard_spec, full_spec),
                         out_specs=(tok_spec, shard_spec, shard_spec, shard_spec, full_spec), check_vma=False)
```

time: 651 us -> 538 us (0.83)
  Pallas kernels: 649 us -> 537 us
    pallas_call x3, Pallas kernels: 649 us -> 537 us  [the longest x1 421 us: backward_reduce(): pl.pallas_call(grads_kernel, grid=(STEPS,), in_specs=[any_spec] * 7, out_...]
where the time goes in v2:
time: 538 us
  Pallas kernels  537 us (100%)
    pallas_call x1, Pallas kernels, backward_reduce(): pl.pallas_call(grads_kernel, grid=(STEPS,), in_specs=[any_spec] * 7, out_...  421 us
    pallas_call x1, Pallas kernels, forward_gather(): pl.pallas_call(gather_kernel, grid=(NF * NT + 1,), in_specs=[any_spec] *...  101 us
    pallas_call x1, Pallas kernels, place_grads(): pl.pallas_call(place_kernel, in_specs=[any_spec, any_spec, pl.BlockSpec(m...  15.4 us

profile of v2, /device:TPU:0, one launch (start us, length us, event | category | flops | bytes accessed | tf_op | source)
XLA Modules:
  0.0 537.7 jit_solution(12416222919984500596)
XLA Ops:
  0.6 100.6 %forward_gather.1 = (bf16[6,4096,1024]{2,1,0:T(8,128)(2,1)}, bf16[4096,768]{1,0:T(8,128)(2,1)}, bf16[12,768,1024]{2,1,0:T(8,128)(2,1)}, bf16[12,512,768]{2,1,0:T(8,128)(2,1)}) custom-call(bf16[4096,768]{1,0:T(8,128)(2,1)} %x_hbm.3, f32[2,768]{1,0:T(2,128)} %gain_hbm.3, bf16[2,192,3072]{2,1,0:T(8,128)(2,1)} %wg_sh.1, bf16[2,192,3072]{2,1,0:T(8,128)(2,1)} %wu_sh.1, ...), custom_call_target="tpu_custom_call" | custom-call | flops 57982058496 | bytes 104857600 | tf_op jit(solution)/shard_map/forward_gather/pallas_call | solution.py:272
  101.3 420.9 %backward_reduce.1 = (bf16[4096,768]{1,0:T(8,128)(2,1)}, bf16[6,4096,512]{2,1,0:T(8,128)(2,1)}, f32[36,2,2,384,256]{4,3,2,1,0:T(8,128)}, f32[36,384,256]{2,1,0:T(8,128)}, f32[2,768]{1,0:T(2,128)}) custom-call(bf16[4096,768]{1,0:T(8,128)(2,1)} %get-tuple-element.17.h1_hbm, bf16[4096,768]{1,0:T(8,128)(2,1)} %x_hbm.3, f32[2,768]{1,0:T(2,128)} %gain_hbm.3, ...), custom_call_target="tpu_custom_call" | custom-call | flops 289910292480 | bytes 335544320 | tf_op jit(solution)/shard_map/backward_reduce/pallas_call | solution.py:690
  522.2 15.4 %place_grads.1 = (f32[2,192,3072]{2,1,0:T(8,128)}, f32[2,192,3072]{2,1,0:T(8,128)}, f32[2,768,768]{2,1,0:T(8,128)}, bf16[4096,768]{1,0:T(8,128)(2,1)}, f32[2,768]{1,0:T(2,128)}) custom-call(f32[36,384,256]{2,1,0:T(8,128)} %get-tuple-element.21.fin, bf16[4096,768]{1,0:T(8,128)(2,1)} %get-tuple-element.22.y_in, f32[2,768]{1,0:T(2,128)} %get-tuple-element.23.gain_in), custom_call_target="tpu_custom_call" | custom-call | bytes 42991616 | tf_op jit(solution)/shard_map/place_grads/pallas_call | solution.py:763

commit v3 on v2

--- a/solution.py
+++ b/solution.py
@@ -28,9 +28,10 @@
 O1, O2, O3, O4, O5, O6, O7 = 1, 4, 6, 9, 13, 17, 18
 BEATS = 2 * (JOBS - 1) + O7 + 1
 MAIN = LAYERS * NF * NT
-STEPS = MAIN + NF * NT
+STEPS = MAIN + NF * NT + 8
 AHEAD = 6
-SLOW = 36
+PACE = 3
+SLOW = 42
 
 
 def dot_nn(a, b):
@@ -476,7 +477,7 @@
     def _():
         dy_copy(step).wait()
 
-    @pl.when(tok == 0)
+    @pl.when(jnp.logical_and(tok == 0, wide < TILES + NF))
     def _():
         wd_copy(wide).wait()
 
@@ -628,8 +629,8 @@
     @pl.when(rest >= 0)
     def _():
         full = rest < SLOW
-        late = 6 * (TILES - 1) + jnp.where(full, lax.div(rest, 3), rest - SLOW + SLOW // 3)
-        due = jnp.logical_or(jnp.logical_not(full), lax.rem(rest, 3) == 0)
+        late = 6 * (TILES - 1) + jnp.where(full, lax.div(rest, PACE), rest - SLOW + SLOW // PACE)
+        due = jnp.logical_or(jnp.logical_not(full), lax.rem(rest, PACE) == 0)
 
         @pl.when(rest + AHEAD < NF * NT)
         def _():
@@ -663,17 +664,19 @@
             gain_out[...] = ((g_zrecv[0] + g_zrecv[1]) + (g_zrecv[2] + g_zrecv[3]))[:LAYERS]
             pltpu.make_async_copy(gain_out, gain_sum_hbm, in_sem.at[1]).start()
 
-        prod_load(rest).wait()
-        dn_all[rows, :] = jnp.where(first_tile, 0.0, dn_all[rows, :]) + dot_nn(ring(rest)[...], wd[slot])
-
-        @pl.when(last_tile)
-        def _():
-            @pl.when(first_tok)
+        @pl.when(rest < NF * NT)
+        def _():
+            prod_load(rest).wait()
+            dn_all[rows, :] = jnp.where(first_tile, 0.0, dn_all[rows, :]) + dot_nn(ring(rest)[...], wd[slot])
+
+            @pl.when(last_tile)
             def _():
-                h1_load.wait()
-
-            n_all[rows, :] = (n_all[rows, :].astype(F32) + dn_all[rows, :]).astype(BF16)
-            y_copy_out(step).start()
+                @pl.when(first_tok)
+                def _():
+                    h1_load.wait()
+
+                n_all[rows, :] = (n_all[rows, :].astype(F32) + dn_all[rows, :]).astype(BF16)
+                y_copy_out(step).start()
 
         @pl.when(step == STEPS - 1)
         def _():

time: 538 us -> 536 us (level)
  no operation moved by 1% of the time
where the time goes in v3:
time: 536 us; the launch traced here: 535 us
  Pallas kernels  535 us (100%)
    pallas_call x1, Pallas kernels, backward_reduce(): pl.pallas_call(grads_kernel, grid=(STEPS,), in_specs=[any_spec] * 7, out_...  419 us
    pallas_call x1, Pallas kernels, forward_gather(): pl.pallas_call(gather_kernel, grid=(NF * NT + 1,), in_specs=[any_spec] *...  101 us
    pallas_call x1, Pallas kernels, place_grads(): pl.pallas_call(place_kernel, in_specs=[any_spec, any_spec, pl.BlockSpec(m...  15.4 us

profile of v3, /device:TPU:0, one launch (start us, length us, event | category | flops | bytes accessed | tf_op | source)
XLA Modules:
  0.0 535.4 jit_solution(10385992995495289696)
XLA Ops:
  0.6 100.6 %forward_gather.1 = (bf16[6,4096,1024]{2,1,0:T(8,128)(2,1)}, bf16[4096,768]{1,0:T(8,128)(2,1)}, bf16[12,768,1024]{2,1,0:T(8,128)(2,1)}, bf16[12,512,768]{2,1,0:T(8,128)(2,1)}) custom-call(bf16[4096,768]{1,0:T(8,128)(2,1)} %x_hbm.3, f32[2,768]{1,0:T(2,128)} %gain_hbm.3, bf16[2,192,3072]{2,1,0:T(8,128)(2,1)} %wg_sh.1, bf16[2,192,3072]{2,1,0:T(8,128)(2,1)} %wu_sh.1, ...), custom_call_target="tpu_custom_call" | custom-call | flops 57982058496 | bytes 104857600 | tf_op jit(solution)/shard_map/forward_gather/pallas_call | solution.py:273
  101.3 418.6 %backward_reduce.1 = (bf16[4096,768]{1,0:T(8,128)(2,1)}, bf16[6,4096,512]{2,1,0:T(8,128)(2,1)}, f32[36,2,2,384,256]{4,3,2,1,0:T(8,128)}, f32[36,384,256]{2,1,0:T(8,128)}, f32[2,768]{1,0:T(2,128)}) custom-call(bf16[4096,768]{1,0:T(8,128)(2,1)} %get-tuple-element.17.h1_hbm, bf16[4096,768]{1,0:T(8,128)(2,1)} %x_hbm.3, f32[2,768]{1,0:T(2,128)} %gain_hbm.3, ...), custom_call_target="tpu_custom_call" | custom-call | flops 289910292480 | bytes 335544320 | tf_op jit(solution)/shard_map/backward_reduce/pallas_call | solution.py:693
  519.8 15.4 %place_grads.1 = (f32[2,192,3072]{2,1,0:T(8,128)}, f32[2,192,3072]{2,1,0:T(8,128)}, f32[2,768,768]{2,1,0:T(8,128)}, bf16[4096,768]{1,0:T(8,128)(2,1)}, f32[2,768]{1,0:T(2,128)}) custom-call(f32[36,384,256]{2,1,0:T(8,128)} %get-tuple-element.21.fin, bf16[4096,768]{1,0:T(8,128)(2,1)} %get-tuple-element.22.y_in, f32[2,768]{1,0:T(2,128)} %get-tuple-element.23.gain_in), custom_call_target="tpu_custom_call" | custom-call | bytes 42991616 | tf_op jit(solution)/shard_map/place_grads/pallas_call | solution.py:766

commit v4 on v3

--- a/solution.py
+++ b/solution.py
@@ -30,6 +30,7 @@
 MAIN = LAYERS * NF * NT
 STEPS = MAIN + NF * NT + 8
 AHEAD = 6
+Z_ORDER = (0, 2, 1)
 PACE = 3
 SLOW = 42
 
@@ -369,16 +370,18 @@
     def stage3(j):
         y_copy(j).wait()
         sum_y[j & 1] = sum_x[j & 1, half_mine, :] + r_y[j & 3]
-        for copy in z_copies(j):
-            copy.start()
+        copies = z_copies(j)
+        for k in Z_ORDER:
+            copies[k].start()
 
     def stage4(j):
         for copy in z_copies(j):
             copy.wait()
         done[j & 7, quarter(zz), :] = ((sum_y[j & 1, rows_of(zz * 48, 48), :] + r_z[j & 3, 0])
                                        + (r_z[j & 3, 1] + r_z[j & 3, 2]))
-        for copy in done_z_copies(j):
-            copy.start()
+        copies = done_z_copies(j)
+        for k in Z_ORDER:
+            copies[k].start()
 
     def stage5(j):
         for copy in done_z_copies(j):

time: 536 us -> 538 us (level)
  no operation moved by 1% of the time
where the time goes in v4:
time: 538 us
  Pallas kernels  537 us (100%)
    pallas_call x1, Pallas kernels, backward_reduce(): pl.pallas_call(grads_kernel, grid=(STEPS,), in_specs=[any_spec] * 7, out_...  421 us
    pallas_call x1, Pallas kernels, forward_gather(): pl.pallas_call(gather_kernel, grid=(NF * NT + 1,), in_specs=[any_spec] *...  101 us
    pallas_call x1, Pallas kernels, place_grads(): pl.pallas_call(place_kernel, in_specs=[any_spec, any_spec, pl.BlockSpec(m...  15.4 us

profile of v4, /device:TPU:0, one launch (start us, length us, event | category | flops | bytes accessed | tf_op | source)
XLA Modules:
  0.0 537.9 jit_solution(11623689803474926255)
XLA Ops:
  0.6 100.6 %forward_gather.1 = (bf16[6,4096,1024]{2,1,0:T(8,128)(2,1)}, bf16[4096,768]{1,0:T(8,128)(2,1)}, bf16[12,768,1024]{2,1,0:T(8,128)(2,1)}, bf16[12,512,768]{2,1,0:T(8,128)(2,1)}) custom-call(bf16[4096,768]{1,0:T(8,128)(2,1)} %x_hbm.3, f32[2,768]{1,0:T(2,128)} %gain_hbm.3, bf16[2,192,3072]{2,1,0:T(8,128)(2,1)} %wg_sh.1, bf16[2,192,3072]{2,1,0:T(8,128)(2,1)} %wu_sh.1, ...), custom_call_target="tpu_custom_call" | custom-call | flops 57982058496 | bytes 104857600 | tf_op jit(solution)/shard_map/forward_gather/pallas_call | solution.py:274
  101.3 421.1 %backward_reduce.1 = (bf16[4096,768]{1,0:T(8,128)(2,1)}, bf16[6,4096,512]{2,1,0:T(8,128)(2,1)}, f32[36,2,2,384,256]{4,3,2,1,0:T(8,128)}, f32[36,384,256]{2,1,0:T(8,128)}, f32[2,768]{1,0:T(2,128)}) custom-call(bf16[4096,768]{1,0:T(8,128)(2,1)} %get-tuple-element.17.h1_hbm, bf16[4096,768]{1,0:T(8,128)(2,1)} %x_hbm.3, f32[2,768]{1,0:T(2,128)} %gain_hbm.3, ...), custom_call_target="tpu_custom_call" | custom-call | flops 289910292480 | bytes 335544320 | tf_op jit(solution)/shard_map/backward_reduce/pallas_call | solution.py:696
  522.4 15.4 %place_grads.1 = (f32[2,192,3072]{2,1,0:T(8,128)}, f32[2,192,3072]{2,1,0:T(8,128)}, f32[2,768,768]{2,1,0:T(8,128)}, bf16[4096,768]{1,0:T(8,128)(2,1)}, f32[2,768]{1,0:T(2,128)}) custom-call(f32[36,384,256]{2,1,0:T(8,128)} %get-tuple-element.21.fin, bf16[4096,768]{1,0:T(8,128)(2,1)} %get-tuple-element.22.y_in, f32[2,768]{1,0:T(2,128)} %get-tuple-element.23.gain_in), custom_call_target="tpu_custom_call" | custom-call | bytes 42991616 | tf_op jit(solution)/shard_map/place_grads/pallas_call | solution.py:769
